TPU v7x, 32 devices: a whole 2x2x4 slice. The times are simulated.
32 devices in a mesh: gx: 4 (over x, core), gy: 4 (over z), gz: 2 (over y).
Axes of the slice: x: 2, y: 2, z: 4, core: 2. Of those that a mesh axis runs over, the one named last changes fastest.
Arguments:
- orbitals: float32 [64, 32, 32, 256], P(None, 'gx', 'gy', 'gz'), may hold values from -6 to 6
- potential: float32 [32, 32, 256], P('gx', 'gy', 'gz'), may hold values from 0 to 0.5
- centre: float32 [64], replicated, may hold values from 3 to 5
- half_width: float32 [64], replicated, may hold values from 3 to 5
Outputs:
- filtered: float32 [64, 32, 32, 256], P(None, 'gx', 'gy', 'gz')
All inputs are finite; a program needn't handle non-finite values.
Results may differ from a plain program's by a relative error of at most 0.00002.
Values sent between devices are 32-bit elements; how exact they have to be, the bound alone decides.
A program may use at most 64 MiB of HBM per device.

v0:
```python
import functools

import jax
import jax.numpy as jnp
from jax import lax
from jax.experimental import pallas as pl
from jax.experimental.pallas import tpu as pltpu
from jax.sharding import PartitionSpec as P

shift_mass = 0.05
jacobi_weight = 2.0 / 3.0
MESH = pl.DeviceIdType.MESH
ORB, FIRST, LEV_A, LEV_B, TWO_A, TWO_B, TWO_C = range(7)


def kernel(sizes, chunks, centre_in, half_width_in, pot_in, orbitals, out, *scratch):
    ext = scratch[0:7]
    second, zsend, zrecv, band_a, band_i, pot_b, d1_b, r1_b, r2_b = scratch[7:16]
    load_sem, store_sem, send_sem, recv_sem = scratch[16:20]
    centre, half_width, pot, small_sem = scratch[20:24]
    packed_out, packed_in = scratch[24:29], scratch[29:34]
    bands, nx, ny, nz = second.shape[2], second.shape[0], second.shape[1], second.shape[3]
    width = bands // chunks
    groups = width // 8
    two_sided = sizes["gz"] > 2
    dims = [(nx, ny, 1)] * 2 + [(nx // 2, ny // 2, 2)] * 2 + [(nx // 4, ny // 4, 4)] * 3
    lane = lax.broadcasted_iota(jnp.int32, (8, nz), 1)
    sub = lax.broadcasted_iota(jnp.int32, (8, nz), 0)

    near = {}
    for axis in ("gx", "gy", "gz"):
        me, n = lax.axis_index(axis), sizes[axis]
        near[axis] = ({axis: lax.rem(me + n - 1, n)}, {axis: lax.rem(me + 1, n)})
    peers = [near["gx"][0], near["gx"][1], near["gy"][0], near["gy"][1], near["gz"][1]]
    if two_sided:
        peers.append(near["gz"][0])

    smalls = [
        pltpu.make_async_copy(src, dst, small_sem.at[j])
        for j, (src, dst) in enumerate(
            [(centre_in, centre), (half_width_in, half_width), (pot_in, pot)]
        )
    ]

    def loads(k):
        rows = pl.ds(pl.multiple_of(k * width, 8), width)

        def line(x, _):
            for y in range(ny):
                pltpu.make_async_copy(
                    orbitals.at[rows, x, y], ext[ORB].at[x + 1, y + 1, rows], load_sem.at[k]
                ).start()
            return 0

        lax.fori_loop(0, nx, line, 0)

    lax.fori_loop(0, chunks, lambda k, c: (loads(k), c)[1], 0)
    for small in smalls:
        small.start()

    barrier = pltpu.get_barrier_semaphore()
    for peer in peers:
        pl.semaphore_signal(barrier, inc=1, device_id=peer, device_id_type=MESH)

    def copies(p, k):
        mx, my, _ = dims[p]
        e = ext[p]
        rows = pl.ds(pl.multiple_of(k * width, 8), width)
        ys, xs = pl.ds(1, my), pl.ds(1, mx)
        if p in (ORB, FIRST):
            moves = [
                (e.at[xs, 1, rows], e.at[xs, my + 1, rows], near["gy"][0]),
                (e.at[xs, my, rows], e.at[xs, 0, rows], near["gy"][1]),
                (e.at[1, ys, rows], e.at[mx + 1, ys, rows], near["gx"][0]),
                (e.at[mx, ys, rows], e.at[0, ys, rows], near["gx"][1]),
            ]
        else:
            share = width if p in (LEV_A, LEV_B) else width // 2
            part = pl.ds(pl.multiple_of(k * share, 8), share)
            sent, got = packed_out[p - LEV_A], packed_in[p - LEV_A]
            moves = [
                (sent.at[j, :, part], got.at[j, :, part], near[axis][side])
                for j, (axis, side) in enumerate(
                    [("gy", 0), ("gy", 1), ("gx", 0), ("gx", 1)]
                )
            ]
        moves.append((zsend.at[p, rows], zrecv.at[p, 0, rows], near["gz"][1]))
        if two_sided:
            moves.append((zsend.at[p, rows], zrecv.at[p, 1, rows], near["gz"][0]))
        return [
            pltpu.make_async_remote_copy(
                src_ref=src,
                dst_ref=dst,
                send_sem=send_sem.at[p, k, j],
                recv_sem=recv_sem.at[p, k, j],
                device_id=to,
                device_id_type=MESH,
            )
            for j, (src, dst, to) in enumerate(moves)
        ]

    def items(p, k):
        mx, my, w = dims[p]
        base = k * width
        if w == 2:
            for i in range(width // 8):
                at = pl.ds(pl.multiple_of(base + 8 * i, 8), 8)
                for pair in range(mx // 2):
                    yield pair, at, [(2 * pair, at), (2 * pair + 1, at)]
        else:
            for i in range(width // 16):
                rows = [pl.ds(pl.multiple_of(base + 16 * i + 8 * h, 8), 8) for h in (0, 1)]
                at = pl.ds(pl.multiple_of(k * (width // 2) + 8 * i, 8), 8)
                for pair in range(mx // 2):
                    yield pair, at, [(2 * pair + c, r) for r in rows for c in (0, 1)]

    def face_cell(p, j, cell, halo):
        mx, my, _ = dims[p]
        if j < 2:
            return (cell + 1, ((my + 1, 0) if halo else (1, my))[j])
        return (((mx + 1, 0) if halo else (1, mx))[j - 2], cell + 1)

    def send(p, k):
        if p not in (ORB, FIRST):
            w = dims[p][2]
            for pair, at, parts in items(p, k):
                for j in range(4):
                    acc = None
                    for spot, (cell, r) in enumerate(parts):
                        cx, cy = face_cell(p, j, cell, False)
                        v = ext[p][cx, cy, r]
                        acc = v if acc is None else jnp.where((lane & (w - 1)) == spot, v, acc)
                    packed_out[p - LEV_A][j, pair, at] = acc
        for copy in copies(p, k):
            copy.start()

    def receive(p, k):
        for copy in copies(p, k):
            copy.wait_recv()
        if p not in (ORB, FIRST):
            w = dims[p][2]
            for pair, at, parts in items(p, k):
                for j in range(4):
                    got = packed_in[p - LEV_A][j, pair, at]
                    for spot, (cell, r) in enumerate(parts):
                        cx, cy = face_cell(p, j, cell, True)
                        v = jnp.where((lane & (w - 1)) == spot, got, 0.0)
                        reach = 1
                        while reach < w:
                            v = v + roll(v, -reach if spot & reach else reach)
                            reach *= 2
                        ext[p][cx, cy, r] = v

    def roll(v, shift):
        return pltpu.roll(v, shift % nz, v.ndim - 1)

    def pack(p, get):
        mx, my, w = dims[p]
        acc = jnp.zeros((8, nz), jnp.float32)
        for x in range(mx):
            for y in range(my):
                at = 2 * w * (x * my + y)
                here = (lane >= at) & (lane < at + 2 * w)
                acc = jnp.where(here, roll(get(x, y), at + w), acc)
        return acc

    def pack_store(p, sl):
        zsend[p, sl] = pack(p, lambda x, y: ext[p][x + 1, y + 1, sl])

    def edges(p, sl):
        w = dims[p][2]
        got = zrecv[p, 0, sl]
        if two_sided:
            got = jnp.where((lane & (2 * w - 1)) < w, got, zrecv[p, 1, sl])
        return got

    def edge_at(p, got, x, y):
        _, my, w = dims[p]
        return roll(got, -(2 * w * (x * my + y)) - w)

    def along_z(v, h, w):
        low = roll(jnp.where(lane[None] >= nz - w, h, v), w)
        high = roll(jnp.where(lane[None] < w, h, v), -w)
        return low + high

    def around(p, sl, got, x):
        _, my, w = dims[p]
        e = ext[p]
        c = e[x + 1, pl.ds(1, my), sl]
        total = e[x, pl.ds(1, my), sl] + e[x + 2, pl.ds(1, my), sl]
        total = total + (e[x + 1, pl.ds(0, my), sl] + e[x + 1, pl.ds(2, my), sl])
        h = jnp.stack([edge_at(p, got, x, y) for y in range(my)])
        return c, total + along_z(c, h, w)

    def pair_sum(v, w):
        even = (lane & (2 * w - 1)) < w
        return v + jnp.where(even, roll(v, -w), roll(v, w))

    def each(body, p_in, p_out):
        def one(k, carry):
            if p_in is not None:
                receive(p_in, k)

            def inner(i, c):
                body(pl.ds(pl.multiple_of(k * width + i * 8, 8), 8))
                return c

            lax.fori_loop(0, groups, inner, 0)
            if p_out is not None:
                send(p_out, k)
            return carry

        lax.fori_loop(0, chunks, one, 0)

    pl.semaphore_wait(barrier, len(peers))

    def start(k, carry):
        rows = pl.ds(pl.multiple_of(k * width, 8), width)
        whole = ext[ORB].at[pl.ds(1, nx), pl.ds(1, ny), rows]
        pltpu.make_async_copy(whole, whole, load_sem.at[k]).wait()

        moves = copies(ORB, k)
        for copy in moves[:4]:
            copy.start()

        def inner(i, c):
            pack_store(ORB, pl.ds(pl.multiple_of(k * width + i * 8, 8), 8))
            return c

        lax.fori_loop(0, groups, inner, 0)
        for copy in moves[4:]:
            copy.start()
        return carry

    lax.fori_loop(0, chunks, start, 0)

    for small in smalls:
        small.wait()
    for g in range(bands // 8):
        m = jnp.zeros((8, nz), jnp.float32)
        s = jnp.ones((8, nz), jnp.float32)
        for j in range(8):
            m = jnp.where(sub == j, centre[g * 8 + j], m)
            s = jnp.where(sub == j, half_width[g * 8 + j], s)
        band_a[pl.ds(g * 8, 8)] = 3.0 - m
        band_i[pl.ds(g * 8, 8)] = 1.0 / s
    for x in range(nx):
        for y in range(ny):
            pot_b[x, y] = jnp.broadcast_to(pot[x, pl.ds(y, 1), :], (8, nz))
    for qx in range(nx // 4):
        for qy in range(ny // 4):
            quad = jnp.zeros((8, nz), jnp.float32)
            for hx in range(2):
                for hy in range(2):
                    x, y = 2 * qx + hx, 2 * qy + hy
                    v = pot_b[2 * x, 2 * y] + pot_b[2 * x + 1, 2 * y]
                    v = v + (pot_b[2 * x, 2 * y + 1] + pot_b[2 * x + 1, 2 * y + 1])
                    one = 0.125 * pair_sum(v, 1)
                    quad = quad + one
                    d1 = 0.75 + one + shift_mass
                    d1_b[x, y] = d1
                    r1_b[x, y] = jacobi_weight / d1
            r2_b[qx, qy] = jacobi_weight / (0.1875 + 0.125 * pair_sum(quad, 2) + shift_mass)

    def step_first(sl):
        got = edges(ORB, sl)
        a, i = band_a[sl], band_i[sl]
        for x in range(nx):
            c, total = around(ORB, sl, got, x)
            ext[FIRST][x + 1, pl.ds(1, ny), sl] = ((pot_b[x] + a) * c - 0.5 * total) * i
        pack_store(FIRST, sl)

    each(step_first, ORB, FIRST)

    def step_second(sl):
        got = edges(FIRST, sl)
        a, i = band_a[sl], 2.0 * band_i[sl]
        for x2 in range(nx // 2):
            pair = None
            for x in (2 * x2, 2 * x2 + 1):
                c, total = around(FIRST, sl, got, x)
                v = ((pot_b[x] + a) * c - 0.5 * total) * i - ext[ORB][x + 1, pl.ds(1, ny), sl]
                second[x, :, sl] = v
                pair = v if pair is None else pair + v
            for y2 in range(ny // 2):
                s = 0.5 * pair_sum(pair[2 * y2] + pair[2 * y2 + 1], 1)
                ext[LEV_A][x2 + 1, y2 + 1, sl] = r1_b[x2, y2] * s
        pack_store(LEV_A, sl)

    each(step_second, FIRST, LEV_A)

    def step_level(sl):
        got = edges(LEV_A, sl)
        for x in range(nx // 2):
            c, total = around(LEV_A, sl, got, x)
            ext[LEV_B][x + 1, pl.ds(1, ny // 2), sl] = (
                (2.0 - jacobi_weight) * c + 0.125 * r1_b[x] * total
            )
        pack_store(LEV_B, sl)

    each(step_level, LEV_A, LEV_B)

    def step_residue(sl):
        got = edges(LEV_B, sl)
        for x2 in range(nx // 4):
            pair = None
            for x in (2 * x2, 2 * x2 + 1):
                c, total = around(LEV_B, sl, got, x)
                d = d1_b[x]
                source = ext[LEV_A][x + 1, pl.ds(1, ny // 2), sl] * (d * (1.0 / jacobi_weight))
                v = source - d * c + 0.125 * total
                pair = v if pair is None else pair + v
            for y2 in range(ny // 4):
                s = 0.5 * pair_sum(pair[2 * y2] + pair[2 * y2 + 1], 2)
                ext[TWO_A][x2 + 1, y2 + 1, sl] = r2_b[x2, y2] * s
        pack_store(TWO_A, sl)

    each(step_residue, LEV_B, TWO_A)

    def step_two(sl):
        got = edges(TWO_A, sl)
        for x in range(nx // 4):
            c, total = around(TWO_A, sl, got, x)
            ext[TWO_B][x + 1, pl.ds(1, ny // 4), sl] = (
                (2.0 - jacobi_weight) * c + 0.03125 * r2_b[x] * total
            )
        pack_store(TWO_B, sl)

    each(step_two, TWO_A, TWO_B)

    def step_two_again(sl):
        got = edges(TWO_B, sl)
        for x in range(nx // 4):
            c, total = around(TWO_B, sl, got, x)
            scaled = ext[TWO_A][x + 1, pl.ds(1, ny // 4), sl]
            ext[TWO_C][x + 1, pl.ds(1, ny // 4), sl] = (
                (1.0 - jacobi_weight) * c + scaled + 0.03125 * r2_b[x] * total
            )
        pack_store(TWO_C, sl)

    each(step_two_again, TWO_B, TWO_C)

    def step_last(sl):
        hx, hy = nx // 2, ny // 2
        fine, coarse = ext[LEV_B], ext[TWO_C]

        def at(x, y):
            return fine[x + 1, y + 1, sl] + coarse[(x + 2) // 2, (y + 2) // 2, sl]

        got_one, got_two = edges(LEV_B, sl), edges(TWO_C, sl)
        for x in range(hx):
            for y in range(hy):
                c = at(x, y)
                total = (at(x - 1, y) + at(x + 1, y)) + (at(x, y - 1) + at(x, y + 1))
                h = edge_at(LEV_B, got_one, x, y) + edge_at(TWO_C, got_two, x // 2, y // 2)
                total = total + along_z(c[None], h[None], 2)[0]
                v = (1.0 - jacobi_weight) * c + ext[LEV_A][x + 1, y + 1, sl]
                v = v + 0.125 * r1_b[x, y] * total
                for i in range(2):
                    for j in range(2):
                        fx, fy = 2 * x + i, 2 * y + j
                        second[fx, fy, sl] = second[fx, fy, sl] + v

    def finish(k, carry):
        rows = pl.ds(pl.multiple_of(k * width, 8), width)
        receive(TWO_C, k)

        def inner(i, c):
            step_last(pl.ds(pl.multiple_of(k * width + i * 8, 8), 8))
            return c

        lax.fori_loop(0, groups, inner, 0)

        def line(x, c):
            for y in range(ny):
                pltpu.make_async_copy(
                    second.at[x, y, rows], out.at[rows, x, y], store_sem.at[k]
                ).start()
            return c

        lax.fori_loop(0, nx, line, 0)
        return carry

    lax.fori_loop(0, chunks, finish, 0)

    def drain(k, carry):
        rows = pl.ds(pl.multiple_of(k * width, 8), width)
        for p in range(7):
            for copy in copies(p, k):
                copy.wait_send()
        whole = second.at[:, :, rows]
        pltpu.make_async_copy(whole, whole, store_sem.at[k]).wait()
        return carry

    lax.fori_loop(0, chunks, drain, 0)


def local(sizes, chunks, orbitals, potential, centre, half_width):
    bands, nx, ny, nz = orbitals.shape

    def f32(*shape):
        return pltpu.VMEM(shape, jnp.float32)

    def padded(cut):
        return f32(nx // cut + 2, ny // cut + 2, bands, nz)

    scratch = [padded(1)] * 2 + [padded(2)] * 2 + [padded(4)] * 3
    scratch += [
        f32(nx, ny, bands, nz),
        f32(7, bands, nz),
        f32(7, 2, bands, nz),
        f32(bands, nz),
        f32(bands, nz),
        f32(nx, ny, 8, nz),
        f32(nx // 2, ny // 2, 8, nz),
        f32(nx // 2, ny // 2, 8, nz),
        f32(nx // 4, ny // 4, 8, nz),
        pltpu.SemaphoreType.DMA((chunks,)),
        pltpu.SemaphoreType.DMA((chunks,)),
        pltpu.SemaphoreType.DMA((7, chunks, 6)),
        pltpu.SemaphoreType.DMA((7, chunks, 6)),
        pltpu.SMEM((bands,), jnp.float32),
        pltpu.SMEM((bands,), jnp.float32),
        f32(nx, ny, nz),
        pltpu.SemaphoreType.DMA((3,)),
    ]
    for _ in range(2):
        scratch += [f32(4, max(nx, ny) // 4, bands, nz)] * 2
        scratch += [f32(4, max(nx, ny) // 8, bands // 2, nz)] * 3
    return pl.pallas_call(
        functools.partial(kernel, sizes, chunks),
        out_shape=jax.ShapeDtypeStruct(orbitals.shape, jnp.float32),
        in_specs=[pl.BlockSpec(memory_space=pltpu.HBM)] * 4,
        out_specs=pl.BlockSpec(memory_space=pl.ANY),
        scratch_shapes=scratch,
        compiler_params=pltpu.CompilerParams(
            collective_id=0, has_side_effects=True, vmem_limit_bytes=48 * 1024 * 1024
        ),
    )(*(pltpu.with_memory_space_constraint(v, pltpu.HBM) for v in (centre, half_width, potential, orbitals)))


def solution(mesh):
    in_specs = (P(None, "gx", "gy", "gz"), P("gx", "gy", "gz"), P(), P())
    out_specs = P(None, "gx", "gy", "gz")
    body = functools.partial(local, dict(mesh.shape), 4)
    return jax.shard_map(body, mesh=mesh, in_specs=in_specs, out_specs=out_specs, check_vma=False)
```

profile of v0, /device:TPU:0, one launch (start us, length us, event | category | flops | bytes accessed | tf_op | source)
XLA Modules:
  0.0 58.7 jit_solution(6878708006087185749)
XLA Ops:
  0.0 57.3 %shard_map.46 = f32[64,8,8,128]{3,2,1,0:T(8,128)S(1)} custom-call(f32[64]{0:T(128)} %centre_in.1, f32[64]{0:T(128)} %half_width_in.1, f32[8,8,128]{2,1,0:T(8,128)} %pot_in.1, f32[64,8,8,128]{3,2,1,0:T(8,128)} %orbitals.1), custom_call_target="tpu_custom_call" | custom-call | tf_op jit(solution)/shard_map/pallas_call | solution.py:430
  57.3 1.3 %copy.6 = f32[64,8,8,128]{3,2,1,0:T(8,128)} copy(f32[64,8,8,128]{3,2,1,0:T(8,128)S(1)} %shard_map.46) | data formatting | bytes 4194304
where the time goes:
time: 58.8 us; the launch traced here: 58.7 us
  Pallas kernels  57.3 us (97%)
  local copies, waits for them, and re-layouts  1.32 us (2%)
    pallas_call x1, Pallas kernels, local(): pl.pallas_call(functools.partial(kernel, sizes, chunks), out_shape=jax.Sh...  57.3 us
    unnamed x1, local copies, waits for them, and re-layouts  1.32 us

commit v1 on v0

v1 whole, which is shorter than its diff:
```python
import functools

import jax
import jax.numpy as jnp
from jax import lax
from jax.experimental import pallas as pl
from jax.experimental.pallas import tpu as pltpu
from jax.sharding import PartitionSpec as P

shift_mass = 0.05
jacobi_weight = 2.0 / 3.0
MESH = pl.DeviceIdType.MESH
ORB, FIRST = range(2)


def kernel(sizes, chunks, centre_in, half_width_in, pot_in, orbitals, out, *scratch):
    fine = scratch[0:2]
    one_a, one_b, two_a, two_b, two_c = scratch[2:7]
    second, zsend, zrecv = scratch[7:10]
    one_edge, one_got, one_halo, two_edge, two_got, last_edge, last_got = scratch[10:17]
    band_a, band_i, pot_b, d1_b, r1_b, r2_b, r_sent, r_got = scratch[17:25]
    load_sem, store_sem, fine_sem, one_sem, two_sem, last_sem, r_sem = scratch[25:32]
    centre, half_width, pot, small_sem = scratch[32:36]
    bands, nx, ny, nz = second.shape[2], second.shape[0], second.shape[1], second.shape[3]
    width = bands // chunks
    groups = width // 8
    pairs = chunks // 2
    mx, my, qx, qy = nx // 2, ny // 2, nx // 4, ny // 4
    sides = 2 if sizes["gz"] > 2 else 1
    lane = lax.broadcasted_iota(jnp.int32, (8, nz), 1)
    sub = lax.broadcasted_iota(jnp.int32, (8, nz), 0)

    near = {}
    for axis in ("gx", "gy", "gz"):
        me, n = lax.axis_index(axis), sizes[axis]
        near[axis] = (lax.rem(me + n - 1, n), lax.rem(me + 1, n))
    zpeers = [near["gz"][1], near["gz"][0]][:sides]
    peers = [{"gx": v} for v in near["gx"]] + [{"gy": v} for v in near["gy"]]
    peers += [{"gz": v} for v in zpeers]

    barrier = pltpu.get_barrier_semaphore()
    for peer in peers:
        pl.semaphore_signal(barrier, inc=1, device_id=peer, device_id_type=MESH)

    smalls = [
        pltpu.make_async_copy(src, dst, small_sem.at[j])
        for j, (src, dst) in enumerate(
            [(centre_in, centre), (half_width_in, half_width), (pot_in, pot)]
        )
    ]
    for small in smalls:
        small.start()

    def loads(k):
        rows = pl.ds(pl.multiple_of(k * width, 8), width)

        def line(x, _):
            for y in range(ny):
                pltpu.make_async_copy(
                    orbitals.at[rows, x, y], fine[ORB].at[x + 1, y + 1, rows], load_sem.at[k]
                ).start()
            return 0

        lax.fori_loop(0, nx, line, 0)

    lax.fori_loop(0, chunks, lambda k, c: (loads(k), c)[1], 0)

    def remote(moves, sems, at):
        return [
            pltpu.make_async_remote_copy(
                src_ref=src,
                dst_ref=dst,
                send_sem=sems.at[(0, *at, j)],
                recv_sem=sems.at[(1, *at, j)],
                device_id=to,
                device_id_type=MESH,
            )
            for j, (src, dst, to) in enumerate(moves)
        ]

    def fine_moves(p, k):
        e = fine[p]
        rows = pl.ds(pl.multiple_of(k * width, 8), width)
        ys, xs = pl.ds(1, ny), pl.ds(1, nx)
        moves = [
            (e.at[xs, 1, rows], e.at[xs, ny + 1, rows], {"gy": near["gy"][0]}),
            (e.at[xs, ny, rows], e.at[xs, 0, rows], {"gy": near["gy"][1]}),
            (e.at[1, ys, rows], e.at[nx + 1, ys, rows], {"gx": near["gx"][0]}),
            (e.at[nx, ys, rows], e.at[0, ys, rows], {"gx": near["gx"][1]}),
        ]
        for s, to in enumerate(zpeers):
            moves.append((zsend.at[p, rows], zrecv.at[p, s, rows], {"gz": to}))
        return remote(moves, fine_sem, (p, k))

    def deep_moves(e, edge, got, sems, k):
        ax, ay = e.shape[0] - 4, e.shape[1] - 4
        rows = pl.ds(pl.multiple_of(k * 8, 8), 8)
        ys, xs = pl.ds(2, ay), pl.ds(2, ax)
        lo, hix, hiy, topx, topy = pl.ds(0, 2), pl.ds(ax, 2), pl.ds(ay, 2), pl.ds(ax + 2, 2), pl.ds(ay + 2, 2)
        two = pl.ds(2, 2)
        (xm, xp), (ym, yp) = near["gx"], near["gy"]
        moves = [
            (e.at[xs, two, rows], e.at[xs, topy, rows], {"gy": ym}),
            (e.at[xs, hiy, rows], e.at[xs, lo, rows], {"gy": yp}),
            (e.at[two, ys, rows], e.at[topx, ys, rows], {"gx": xm}),
            (e.at[hix, ys, rows], e.at[lo, ys, rows], {"gx": xp}),
            (e.at[2, 2, rows], e.at[ax + 2, ay + 2, rows], {"gx": xm, "gy": ym}),
            (e.at[ax + 1, 2, rows], e.at[1, ay + 2, rows], {"gx": xp, "gy": ym}),
            (e.at[2, ay + 1, rows], e.at[ax + 2, 1, rows], {"gx": xm, "gy": yp}),
            (e.at[ax + 1, ay + 1, rows], e.at[1, 1, rows], {"gx": xp, "gy": yp}),
        ]
        for s, z in enumerate(zpeers):
            for j, to in enumerate([{}, {"gx": xp}, {"gx": xm}, {"gy": yp}, {"gy": ym}]):
                moves.append((edge.at[rows], got.at[s, j, rows], {"gz": z, **to}))
        return remote(moves, sems, (k,))

    def last_moves(k):
        e = two_c
        rows = pl.ds(pl.multiple_of(k * 8, 8), 8)
        ys, xs = pl.ds(1, qy), pl.ds(1, qx)
        moves = [
            (e.at[xs, 1, rows], e.at[xs, qy + 1, rows], {"gy": near["gy"][0]}),
            (e.at[xs, qy, rows], e.at[xs, 0, rows], {"gy": near["gy"][1]}),
            (e.at[1, ys, rows], e.at[qx + 1, ys, rows], {"gx": near["gx"][0]}),
            (e.at[qx, ys, rows], e.at[0, ys, rows], {"gx": near["gx"][1]}),
        ]
        for s, to in enumerate(zpeers):
            moves.append((last_edge.at[rows], last_got.at[s, rows], {"gz": to}))
        return remote(moves, last_sem, (k,))

    def r_moves():
        moves = [
            (r_sent.at[0], r_got.at[1], {"gx": near["gx"][0]}),
            (r_sent.at[1], r_got.at[0], {"gx": near["gx"][1]}),
            (r_sent.at[2], r_got.at[3], {"gy": near["gy"][0]}),
            (r_sent.at[3], r_got.at[2], {"gy": near["gy"][1]}),
        ]
        for s, to in enumerate(zpeers):
            moves.append((r_sent.at[4], r_got.at[4 + s], {"gz": to}))
        return remote(moves, r_sem, ())

    def one_moves(k):
        return deep_moves(one_a, one_edge, one_got, one_sem, k)

    def two_moves(k):
        return deep_moves(two_a, two_edge, two_got, two_sem, k)

    def go(moves):
        for copy in moves:
            copy.start()

    def arrive(moves):
        for copy in moves:
            copy.wait_recv()

    def leave(moves):
        for copy in moves:
            copy.wait_send()

    def roll(v, shift):
        return pltpu.roll(v, shift % nz, v.ndim - 1)

    def pack(get, ax, ay, w):
        acc = jnp.zeros((8, nz), jnp.float32)
        for x in range(ax):
            for y in range(ay):
                at = 2 * w * (x * ay + y)
                here = (lane >= at) & (lane < at + 2 * w)
                acc = jnp.where(here, roll(get(x, y), at + w), acc)
        return acc

    def edge_at(got, spot, w):
        return roll(got, -(2 * w * spot) - w)

    def join(got, w):
        if sides == 1:
            return got(0)
        return jnp.where((lane & (2 * w - 1)) < w, got(0), got(1))

    def along_z(v, h, w):
        low = roll(jnp.where(lane >= nz - w, h, v), w)
        high = roll(jnp.where(lane < w, h, v), -w)
        return low + high

    def pair_sum(v, w):
        even = (lane & (2 * w - 1)) < w
        return v + jnp.where(even, roll(v, -w), roll(v, w))

    def sweep_edges(own, ends, r, ax, ay, w, coupling):
        cell = w // 2
        mid, xm, xp, ym, yp = ends
        sy, sx = 2 * w, 2 * w * ay
        spot = lane // sy
        yi, xi = spot % ay, spot // ay
        z = jnp.where(
            (lane & (2 * w - 1)) >= w,
            roll(mid, -cell) + roll(own, cell),
            roll(mid, cell) + roll(own, -cell),
        )
        total = z + jnp.where(yi == ay - 1, roll(yp, sy * (ay - 1)), roll(mid, -sy))
        total = total + jnp.where(yi == 0, roll(ym, -sy * (ay - 1)), roll(mid, sy))
        total = total + jnp.where(xi == ax - 1, roll(xp, sx * (ax - 1)), roll(mid, -sx))
        total = total + jnp.where(xi == 0, roll(xm, -sx * (ax - 1)), roll(mid, sx))
        return (2.0 - jacobi_weight) * mid + coupling * r * total

    def sweep_wide(src, dst, ends, r_at, rows, ax, ay, w, coupling):
        mid, xm, xp, ym, yp = ends
        cells = [(x, y, mid, x * ay + y) for x in range(ax) for y in range(ay)]
        cells += [(-1, y, xm, (ax - 1) * ay + y) for y in range(ay)]
        cells += [(ax, y, xp, y) for y in range(ay)]
        cells += [(x, -1, ym, x * ay + ay - 1) for x in range(ax)]
        cells += [(x, ay, yp, x * ay) for x in range(ax)]
        for x, y, got, spot in cells:
            c = src[x + 2, y + 2, rows]
            total = (src[x + 1, y + 2, rows] + src[x + 3, y + 2, rows]) + (
                src[x + 2, y + 1, rows] + src[x + 2, y + 3, rows]
            )
            total = total + along_z(c, edge_at(got, spot, w), w // 2)
            dst[x + 1, y + 1, rows] = (2.0 - jacobi_weight) * c + coupling * r_at(x, y) * total

    def total_of(e, x, y, rows, h, w):
        c = e[x + 1, y + 1, rows]
        total = (e[x, y + 1, rows] + e[x + 2, y + 1, rows]) + (
            e[x + 1, y, rows] + e[x + 1, y + 2, rows]
        )
        return c, total + along_z(c, h, w)

    def around(p, sl, got, x):
        e = fine[p]
        c = e[x + 1, pl.ds(1, ny), sl]
        total = e[x, pl.ds(1, ny), sl] + e[x + 2, pl.ds(1, ny), sl]
        total = total + (e[x + 1, pl.ds(0, ny), sl] + e[x + 1, pl.ds(2, ny), sl])
        h = jnp.stack([edge_at(got, x * ny + y, 1) for y in range(ny)])
        low = roll(jnp.where(lane[None] >= nz - 1, h, c), 1)
        high = roll(jnp.where(lane[None] < 1, h, c), -1)
        return c, total + (low + high)

    def fine_edges(p, sl):
        return join(lambda s: zrecv[p, s, sl], 1)

    def fine_pack(p, sl):
        zsend[p, sl] = pack(lambda x, y: fine[p][x + 1, y + 1, sl], nx, ny, 1)

    def slab(k, i):
        return pl.ds(pl.multiple_of(k * width + i * 8, 8), 8)

    for small in smalls:
        small.wait()
    for g in range(bands // 8):
        m = jnp.zeros((8, nz), jnp.float32)
        s = jnp.ones((8, nz), jnp.float32)
        for j in range(8):
            m = jnp.where(sub == j, centre[g * 8 + j], m)
            s = jnp.where(sub == j, half_width[g * 8 + j], s)
        band_a[pl.ds(g * 8, 8)] = 3.0 - m
        band_i[pl.ds(g * 8, 8)] = 1.0 / s
    for x in range(nx):
        for y in range(ny):
            pot_b[x, y] = jnp.broadcast_to(pot[x, pl.ds(y, 1), :], (8, nz))
    for x2 in range(qx):
        for y2 in range(qy):
            quad = jnp.zeros((8, nz), jnp.float32)
            for hx in range(2):
                for hy in range(2):
                    x, y = 2 * x2 + hx, 2 * y2 + hy
                    v = pot_b[2 * x, 2 * y] + pot_b[2 * x + 1, 2 * y]
                    v = v + (pot_b[2 * x, 2 * y + 1] + pot_b[2 * x + 1, 2 * y + 1])
                    one = 0.125 * pair_sum(v, 1)
                    quad = quad + one
                    d1 = 0.75 + one + shift_mass
                    d1_b[x, y] = d1
                    r1_b[x + 1, y + 1] = jacobi_weight / d1
            r2_b[x2 + 1, y2 + 1] = jacobi_weight / (0.1875 + 0.125 * pair_sum(quad, 2) + shift_mass)
    for j, (x, y) in enumerate([(0, None), (mx - 1, None), (None, 0), (None, my - 1)]):
        for i in range(my if y is None else mx):
            cx, cy = (x, i) if y is None else (i, y)
            r_sent[j, pl.ds(i, 1)] = r1_b[cx + 1, cy + 1][0:1]
    for j, (x, y) in enumerate([(0, None), (qx - 1, None), (None, 0), (None, qy - 1)]):
        base = my if y is None else mx
        for i in range(qy if y is None else qx):
            cx, cy = (x, i) if y is None else (i, y)
            r_sent[j, pl.ds(base + i, 1)] = r2_b[cx + 1, cy + 1][0:1]
    r_sent[4, pl.ds(0, 1)] = pack(lambda x, y: r1_b[x + 1, y + 1], mx, my, 4)[0:1]
    r_sent[4, pl.ds(1, 1)] = pack(lambda x, y: r2_b[x + 1, y + 1], qx, qy, 8)[0:1]

    def ready(k, carry):
        rows = pl.ds(pl.multiple_of(k * width, 8), width)
        whole = fine[ORB].at[pl.ds(1, nx), pl.ds(1, ny), rows]
        pltpu.make_async_copy(whole, whole, load_sem.at[k]).wait()

        def inner(i, c):
            fine_pack(ORB, slab(k, i))
            return c

        lax.fori_loop(0, groups, inner, 0)
        return carry

    lax.fori_loop(0, chunks, ready, 0)

    pl.semaphore_wait(barrier, len(peers))
    lax.fori_loop(0, chunks, lambda k, c: (go(fine_moves(ORB, k)), c)[1], 0)
    go(r_moves())

    def step_first(k, carry):
        arrive(fine_moves(ORB, k))

        def inner(i, c):
            sl = slab(k, i)
            got = fine_edges(ORB, sl)
            a, f = band_a[sl], band_i[sl]
            for x in range(nx):
                v, total = around(ORB, sl, got, x)
                fine[FIRST][x + 1, pl.ds(1, ny), sl] = ((pot_b[x] + a) * v - 0.5 * total) * f
            fine_pack(FIRST, sl)
            return c

        lax.fori_loop(0, groups, inner, 0)
        go(fine_moves(FIRST, k))
        return carry

    lax.fori_loop(0, chunks, step_first, 0)

    arrive(r_moves())
    for i in range(my):
        for j, x in ((0, 0), (1, mx + 1)):
            r1_b[x, i + 1] = jnp.broadcast_to(r_got[j, pl.ds(i, 1)], (8, nz))
    for i in range(mx):
        for j, y in ((2, 0), (3, my + 1)):
            r1_b[i + 1, y] = jnp.broadcast_to(r_got[j, pl.ds(i, 1)], (8, nz))
    for i in range(qy):
        for j, x in ((0, 0), (1, qx + 1)):
            r2_b[x, i + 1] = jnp.broadcast_to(r_got[j, pl.ds(my + i, 1)], (8, nz))
    for i in range(qx):
        for j, y in ((2, 0), (3, qy + 1)):
            r2_b[i + 1, y] = jnp.broadcast_to(r_got[j, pl.ds(mx + i, 1)], (8, nz))

    def r_edge(row, w):
        return join(lambda s: jnp.broadcast_to(r_got[4 + s, pl.ds(row, 1)], (8, nz)), w)

    def step_second(k, carry):
        arrive(fine_moves(FIRST, k))
        packed = pl.ds(pl.multiple_of(k * 8, 8), 8)

        def inner(i, c):
            sl = slab(k, i)
            mine = (lane & 1) == i
            got = fine_edges(FIRST, sl)
            a, f = band_a[sl], 2.0 * band_i[sl]
            for x2 in range(mx):
                both = None
                for x in (2 * x2, 2 * x2 + 1):
                    v, total = around(FIRST, sl, got, x)
                    v = ((pot_b[x] + a) * v - 0.5 * total) * f - fine[ORB][x + 1, pl.ds(1, ny), sl]
                    second[x, :, sl] = v
                    both = v if both is None else both + v
                for y2 in range(my):
                    s = 0.5 * pair_sum(both[2 * y2] + both[2 * y2 + 1], 1)
                    one_a[x2 + 2, y2 + 2, packed] = jnp.where(
                        mine, r1_b[x2 + 1, y2 + 1] * s, one_a[x2 + 2, y2 + 2, packed]
                    )
            return c

        lax.fori_loop(0, groups, inner, 0)
        one_edge[packed] = pack(lambda x, y: one_a[x + 2, y + 2, packed], mx, my, 4)
        go(one_moves(k))
        return carry

    lax.fori_loop(0, chunks, step_second, 0)

    def step_residue(k, carry):
        arrive(one_moves(k))
        packed = pl.ds(pl.multiple_of(k * 8, 8), 8)
        rows = pl.ds(pl.multiple_of(lax.div(k, 2) * 8, 8), 8)
        mine = ((lane >> 1) & 1) == lax.rem(k, 2)
        ends = [join(lambda s, j=j: one_got[s, j, packed], 4) for j in range(5)]
        halo = sweep_edges(one_edge[packed], ends, r_edge(0, 4), mx, my, 4, 0.125)
        one_halo[packed] = halo
        sweep_wide(
            one_a, one_b, ends, lambda x, y: r1_b[x + 1, y + 1], packed, mx, my, 4, 0.125
        )
        for x2 in range(qx):
            for y2 in range(qy):
                acc = None
                for x in (2 * x2, 2 * x2 + 1):
                    for y in (2 * y2, 2 * y2 + 1):
                        h = edge_at(halo, x * my + y, 4)
                        c, total = total_of(one_b, x, y, packed, h, 2)
                        d = d1_b[x, y]
                        source = one_a[x + 2, y + 2, packed] * (d * (1.0 / jacobi_weight))
                        v = source - d * c + 0.125 * total
                        acc = v if acc is None else acc + v
                s = 0.5 * pair_sum(acc, 2)
                two_a[x2 + 2, y2 + 2, rows] = jnp.where(
                    mine, r2_b[x2 + 1, y2 + 1] * s, two_a[x2 + 2, y2 + 2, rows]
                )
        return carry

    def pair_residue(k, carry):
        lax.fori_loop(2 * k, 2 * k + 2, step_residue, 0)
        rows = pl.ds(pl.multiple_of(k * 8, 8), 8)
        two_edge[rows] = pack(lambda x, y: two_a[x + 2, y + 2, rows], qx, qy, 8)
        go(two_moves(k))
        return carry

    lax.fori_loop(0, pairs, pair_residue, 0)

    def step_two(k, carry):
        arrive(two_moves(k))
        rows = pl.ds(pl.multiple_of(k * 8, 8), 8)
        ends = [join(lambda s, j=j: two_got[s, j, rows], 8) for j in range(5)]
        halo = sweep_edges(two_edge[rows], ends, r_edge(1, 8), qx, qy, 8, 0.03125)
        sweep_wide(
            two_a, two_b, ends, lambda x, y: r2_b[x + 1, y + 1], rows, qx, qy, 8, 0.03125
        )
        for x in range(qx):
            for y in range(qy):
                c, total = total_of(two_b, x, y, rows, edge_at(halo, x * qy + y, 8), 4)
                two_c[x + 1, y + 1, rows] = (
                    (1.0 - jacobi_weight) * c
                    + two_a[x + 2, y + 2, rows]
                    + 0.03125 * r2_b[x + 1, y + 1] * total
                )
        last_edge[rows] = pack(lambda x, y: two_c[x + 1, y + 1, rows], qx, qy, 4)
        go(last_moves(k))
        return carry

    lax.fori_loop(0, pairs, step_two, 0)

    def step_last(k, half):
        rows = pl.ds(pl.multiple_of(k * 8, 8), 8)
        packed = pl.ds(pl.multiple_of(k * 16 + half * 8, 8), 8)
        left = (lane & 2) == 0

        def spread(v):
            return jnp.where(left, v, roll(v, 2)) if half == 0 else jnp.where(left, roll(v, -2), v)

        coarse = {}
        for x in range(-1, qx + 1):
            for y in range(-1, qy + 1):
                if 0 <= x < qx or 0 <= y < qy:
                    coarse[x, y] = spread(two_c[x + 1, y + 1, rows])
        got = join(lambda s: last_got[s, rows], 4)
        ends = {
            (x, y): spread(edge_at(got, x * qy + y, 4)) for x in range(qx) for y in range(qy)
        }
        halo = one_halo[packed]

        def at(x, y):
            return one_b[x + 1, y + 1, packed] + coarse[(x + 2) // 2 - 1, (y + 2) // 2 - 1]

        for x in range(mx):
            for y in range(my):
                c = at(x, y)
                total = (at(x - 1, y) + at(x + 1, y)) + (at(x, y - 1) + at(x, y + 1))
                h = edge_at(halo, x * my + y, 4) + ends[x // 2, y // 2]
                total = total + along_z(c, h, 2)
                v = (1.0 - jacobi_weight) * c + one_a[x + 2, y + 2, packed]
                v = v + 0.125 * r1_b[x + 1, y + 1] * total
                odd = (lane & 1) == 1
                for i, w in enumerate((jnp.where(odd, roll(v, 1), v), jnp.where(odd, v, roll(v, -1)))):
                    sl = slab(2 * k + half, i)
                    for hx in range(2):
                        for hy in range(2):
                            fx, fy = 2 * x + hx, 2 * y + hy
                            second[fx, fy, sl] = second[fx, fy, sl] + w

    def finish(k, carry):
        arrive(last_moves(k))
        for half in range(2):
            step_last(k, half)
            rows = pl.ds(pl.multiple_of((2 * k + half) * width, 8), width)

            def line(x, c):
                for y in range(ny):
                    pltpu.make_async_copy(
                        second.at[x, y, rows], out.at[rows, x, y], store_sem.at[2 * k + half]
                    ).start()
                return c

            lax.fori_loop(0, nx, line, 0)
        return carry

    lax.fori_loop(0, pairs, finish, 0)

    def drain(k, carry):
        rows = pl.ds(pl.multiple_of(k * width, 8), width)
        for p in (ORB, FIRST):
            leave(fine_moves(p, k))
        leave(one_moves(k))
        whole = second.at[:, :, rows]
        pltpu.make_async_copy(whole, whole, store_sem.at[k]).wait()
        return carry

    lax.fori_loop(0, chunks, drain, 0)

    def drain_pair(k, carry):
        leave(two_moves(k))
        leave(last_moves(k))
        return carry

    lax.fori_loop(0, pairs, drain_pair, 0)
    leave(r_moves())


def local(sizes, chunks, orbitals, potential, centre, half_width):
    bands, nx, ny, nz = orbitals.shape
    sides = 2 if sizes["gz"] > 2 else 1
    pairs = chunks // 2

    def f32(*shape):
        return pltpu.VMEM(shape, jnp.float32)

    def padded(cut, halo):
        return f32(nx // cut + 2 * halo, ny // cut + 2 * halo, bands if cut == 1 else bands // cut, nz)

    dma = pltpu.SemaphoreType.DMA
    deep = 8 + 5 * sides
    scratch = [padded(1, 1)] * 2 + [padded(2, 2), padded(2, 1), padded(4, 2), padded(4, 1), padded(4, 1)]
    scratch += [
        f32(nx, ny, bands, nz),
        f32(2, bands, nz),
        f32(2, sides, bands, nz),
        f32(bands // 2, nz),
        f32(sides, 5, bands // 2, nz),
        f32(bands // 2, nz),
        f32(bands // 4, nz),
        f32(sides, 5, bands // 4, nz),
        f32(bands // 4, nz),
        f32(sides, bands // 4, nz),
        f32(bands, nz),
        f32(bands, nz),
        f32(nx, ny, 8, nz),
        f32(nx // 2, ny // 2, 8, nz),
        f32(nx // 2 + 2, ny // 2 + 2, 8, nz),
        f32(nx // 4 + 2, ny // 4 + 2, 8, nz),
        f32(5, 8, nz),
        f32(4 + sides, 8, nz),
        dma((chunks,)),
        dma((chunks,)),
        dma((2, 2, chunks, 4 + sides)),
        dma((2, chunks, deep)),
        dma((2, pairs, deep)),
        dma((2, pairs, 4 + sides)),
        dma((2, 4 + sides)),
        pltpu.SMEM((bands,), jnp.float32),
        pltpu.SMEM((bands,), jnp.float32),
        f32(nx, ny, nz),
        dma((3,)),
    ]
    return pl.pallas_call(
        functools.partial(kernel, sizes, chunks),
        out_shape=jax.ShapeDtypeStruct(orbitals.shape, jnp.float32),
        in_specs=[pl.BlockSpec(memory_space=pltpu.HBM)] * 4,
        out_specs=pl.BlockSpec(memory_space=pl.ANY),
        scratch_shapes=scratch,
        compiler_params=pltpu.CompilerParams(
            collective_id=0, has_side_effects=True, vmem_limit_bytes=48 * 1024 * 1024
        ),
    )(*(pltpu.with_memory_space_constraint(v, pltpu.HBM) for v in (centre, half_width, potential, orbitals)))


def solution(mesh):
    in_specs = (P(None, "gx", "gy", "gz"), P("gx", "gy", "gz"), P(), P())
    out_specs = P(None, "gx", "gy", "gz")
    body = functools.partial(local, dict(mesh.shape), 4)
    return jax.shard_map(body, mesh=mesh, in_specs=in_specs, out_specs=out_specs, check_vma=False)
```

time: 58.8 us -> 54.3 us (0.923)
  Pallas kernels: 57.3 us -> 52.7 us
    pallas_call x1, Pallas kernels: 57.3 us -> 52.7 us  [local(): pl.pallas_call(functools.partial(kernel, sizes, chunks), out_shape=jax.Sh...]
where the time goes in v1:
time: 54.3 us; the launch traced here: 54 us
  Pallas kernels  52.7 us (97%)
  local copies, waits for them, and re-layouts  1.32 us (2%)
    pallas_call x1, Pallas kernels, local(): pl.pallas_call(functools.partial(kernel, sizes, chunks), out_shape=jax.Sh...  52.7 us
    unnamed x1, local copies, waits for them, and re-layouts  1.32 us

profile of v1, /device:TPU:0, one launch (start us, length us, event | category | flops | bytes accessed | tf_op | source)
XLA Modules:
  0.0 54.0 jit_solution(1209582065361824642)
XLA Ops:
  0.0 52.7 %shard_map.46 = f32[64,8,8,128]{3,2,1,0:T(8,128)S(1)} custom-call(f32[64]{0:T(128)} %centre_in.1, f32[64]{0:T(128)} %half_width_in.1, f32[8,8,128]{2,1,0:T(8,128)} %pot_in.1, f32[64,8,8,128]{3,2,1,0:T(8,128)} %orbitals.1), custom_call_target="tpu_custom_call" | custom-call | tf_op jit(solution)/shard_map/pallas_call | solution.py:550
  52.7 1.3 %copy.6 = f32[64,8,8,128]{3,2,1,0:T(8,128)} copy(f32[64,8,8,128]{3,2,1,0:T(8,128)S(1)} %shard_map.46) | data formatting | bytes 4194304

commit v2 on v1

--- a/solution.py
+++ b/solution.py
@@ -1,4 +1,5 @@
 import functools
+import math
 
 import jax
 import jax.numpy as jnp
@@ -13,20 +14,22 @@
 ORB, FIRST = range(2)
 
 
-def kernel(sizes, chunks, centre_in, half_width_in, pot_in, orbitals, out, *scratch):
+def kernel(sizes, chunks, centre_in, half_width_in, pot_in, orbitals, second, *scratch):
     fine = scratch[0:2]
     one_a, one_b, two_a, two_b, two_c = scratch[2:7]
-    second, zsend, zrecv = scratch[7:10]
-    one_edge, one_got, one_halo, two_edge, two_got, last_edge, last_got = scratch[10:17]
-    band_a, band_i, pot_b, d1_b, r1_b, r2_b, r_sent, r_got = scratch[17:25]
-    load_sem, store_sem, fine_sem, one_sem, two_sem, last_sem, r_sem = scratch[25:32]
-    centre, half_width, pot, small_sem = scratch[32:36]
+    zsend, zrecv = scratch[7:9]
+    one_edge, one_got, one_halo, two_edge, two_got, last_edge, last_got = scratch[9:16]
+    band_a, band_i, pot_b, d1_b, r1_b, r2_b, r_sent, r_got = scratch[16:24]
+    load_sem, send_sem, recv_sem, tally = scratch[24:28]
+    centre, half_width, pot, small_sem = scratch[28:32]
     bands, nx, ny, nz = second.shape[2], second.shape[0], second.shape[1], second.shape[3]
     width = bands // chunks
     groups = width // 8
     pairs = chunks // 2
     mx, my, qx, qy = nx // 2, ny // 2, nx // 4, ny // 4
     sides = 2 if sizes["gz"] > 2 else 1
+    at_one, at_two = 2 * chunks, 3 * chunks
+    at_last, at_r = at_two + pairs, at_two + 2 * pairs
     lane = lax.broadcasted_iota(jnp.int32, (8, nz), 1)
     sub = lax.broadcasted_iota(jnp.int32, (8, nz), 0)
 
@@ -65,18 +68,29 @@
 
     lax.fori_loop(0, chunks, lambda k, c: (loads(k), c)[1], 0)
 
-    def remote(moves, sems, at):
-        return [
+    def tiles(moves):
+        return sum(math.prod(src.shape) for src, _, _ in moves) // (8 * nz)
+
+    def take(n, sem):
+        whole = tally.at[pl.ds(0, n)]
+        pltpu.make_async_copy(whole, whole, sem).wait()
+
+    def go(moves, sent, got):
+        for src, dst, to in moves:
             pltpu.make_async_remote_copy(
                 src_ref=src,
                 dst_ref=dst,
-                send_sem=sems.at[(0, *at, j)],
-                recv_sem=sems.at[(1, *at, j)],
+                send_sem=send_sem.at[sent],
+                recv_sem=recv_sem.at[got],
                 device_id=to,
                 device_id_type=MESH,
-            )
-            for j, (src, dst, to) in enumerate(moves)
-        ]
+            ).start()
+
+    def arrive(moves, got):
+        take(tiles(moves), recv_sem.at[got])
+
+    def leave(moves, times, sent):
+        take(times * tiles(moves), send_sem.at[sent])
 
     def fine_moves(p, k):
         e = fine[p]
@@ -90,9 +104,9 @@
         ]
         for s, to in enumerate(zpeers):
             moves.append((zsend.at[p, rows], zrecv.at[p, s, rows], {"gz": to}))
-        return remote(moves, fine_sem, (p, k))
-
-    def deep_moves(e, edge, got, sems, k):
+        return moves
+
+    def deep_moves(e, edge, got, k):
         ax, ay = e.shape[0] - 4, e.shape[1] - 4
         rows = pl.ds(pl.multiple_of(k * 8, 8), 8)
         ys, xs = pl.ds(2, ay), pl.ds(2, ax)
@@ -112,7 +126,7 @@
         for s, z in enumerate(zpeers):
             for j, to in enumerate([{}, {"gx": xp}, {"gx": xm}, {"gy": yp}, {"gy": ym}]):
                 moves.append((edge.at[rows], got.at[s, j, rows], {"gz": z, **to}))
-        return remote(moves, sems, (k,))
+        return moves
 
     def last_moves(k):
         e = two_c
@@ -126,7 +140,7 @@
         ]
         for s, to in enumerate(zpeers):
             moves.append((last_edge.at[rows], last_got.at[s, rows], {"gz": to}))
-        return remote(moves, last_sem, (k,))
+        return moves
 
     def r_moves():
         moves = [
@@ -137,25 +151,13 @@
         ]
         for s, to in enumerate(zpeers):
             moves.append((r_sent.at[4], r_got.at[4 + s], {"gz": to}))
-        return remote(moves, r_sem, ())
+        return moves
 
     def one_moves(k):
-        return deep_moves(one_a, one_edge, one_got, one_sem, k)
+        return deep_moves(one_a, one_edge, one_got, k)
 
     def two_moves(k):
-        return deep_moves(two_a, two_edge, two_got, two_sem, k)
-
-    def go(moves):
-        for copy in moves:
-            copy.start()
-
-    def arrive(moves):
-        for copy in moves:
-            copy.wait_recv()
-
-    def leave(moves):
-        for copy in moves:
-            copy.wait_send()
+        return deep_moves(two_a, two_edge, two_got, k)
 
     def roll(v, shift):
         return pltpu.roll(v, shift % nz, v.ndim - 1)
@@ -243,6 +245,27 @@
 
     def slab(k, i):
         return pl.ds(pl.multiple_of(k * width + i * 8, 8), 8)
+
+    def ready(k, carry):
+        rows = pl.ds(pl.multiple_of(k * width, 8), width)
+        whole = fine[ORB].at[pl.ds(1, nx), pl.ds(1, ny), rows]
+        pltpu.make_async_copy(whole, whole, load_sem.at[k]).wait()
+        return carry
+
+    lax.fori_loop(0, chunks, ready, 0)
+    pl.semaphore_wait(barrier, len(peers))
+    lax.fori_loop(0, chunks, lambda k, c: (go(fine_moves(ORB, k)[:4], 0, k), c)[1], 0)
+
+    def start_z(k, carry):
+        def inner(i, c):
+            fine_pack(ORB, slab(k, i))
+            return c
+
+        lax.fori_loop(0, groups, inner, 0)
+        go(fine_moves(ORB, k)[4:], 0, k)
+        return carry
+
+    lax.fori_loop(0, chunks, start_z, 0)
 
     for small in smalls:
         small.wait()
@@ -283,26 +306,10 @@
     r_sent[4, pl.ds(0, 1)] = pack(lambda x, y: r1_b[x + 1, y + 1], mx, my, 4)[0:1]
     r_sent[4, pl.ds(1, 1)] = pack(lambda x, y: r2_b[x + 1, y + 1], qx, qy, 8)[0:1]
 
-    def ready(k, carry):
-        rows = pl.ds(pl.multiple_of(k * width, 8), width)
-        whole = fine[ORB].at[pl.ds(1, nx), pl.ds(1, ny), rows]
-        pltpu.make_async_copy(whole, whole, load_sem.at[k]).wait()
-
-        def inner(i, c):
-            fine_pack(ORB, slab(k, i))
-            return c
-
-        lax.fori_loop(0, groups, inner, 0)
-        return carry
-
-    lax.fori_loop(0, chunks, ready, 0)
-
-    pl.semaphore_wait(barrier, len(peers))
-    lax.fori_loop(0, chunks, lambda k, c: (go(fine_moves(ORB, k)), c)[1], 0)
-    go(r_moves())
+    go(r_moves(), 5, at_r)
 
     def step_first(k, carry):
-        arrive(fine_moves(ORB, k))
+        arrive(fine_moves(ORB, k), k)
 
         def inner(i, c):
             sl = slab(k, i)
@@ -315,12 +322,12 @@
             return c
 
         lax.fori_loop(0, groups, inner, 0)
-        go(fine_moves(FIRST, k))
+        go(fine_moves(FIRST, k), 1, chunks + k)
         return carry
 
     lax.fori_loop(0, chunks, step_first, 0)
 
-    arrive(r_moves())
+    arrive(r_moves(), at_r)
     for i in range(my):
         for j, x in ((0, 0), (1, mx + 1)):
             r1_b[x, i + 1] = jnp.broadcast_to(r_got[j, pl.ds(i, 1)], (8, nz))
@@ -338,7 +345,7 @@
         return join(lambda s: jnp.broadcast_to(r_got[4 + s, pl.ds(row, 1)], (8, nz)), w)
 
     def step_second(k, carry):
-        arrive(fine_moves(FIRST, k))
+        arrive(fine_moves(FIRST, k), chunks + k)
         packed = pl.ds(pl.multiple_of(k * 8, 8), 8)
 
         def inner(i, c):
@@ -362,13 +369,13 @@
 
         lax.fori_loop(0, groups, inner, 0)
         one_edge[packed] = pack(lambda x, y: one_a[x + 2, y + 2, packed], mx, my, 4)
-        go(one_moves(k))
+        go(one_moves(k), 2, at_one + k)
         return carry
 
     lax.fori_loop(0, chunks, step_second, 0)
 
     def step_residue(k, carry):
-        arrive(one_moves(k))
+        arrive(one_moves(k), at_one + k)
         packed = pl.ds(pl.multiple_of(k * 8, 8), 8)
         rows = pl.ds(pl.multiple_of(lax.div(k, 2) * 8, 8), 8)
         mine = ((lane >> 1) & 1) == lax.rem(k, 2)
@@ -399,13 +406,13 @@
         lax.fori_loop(2 * k, 2 * k + 2, step_residue, 0)
         rows = pl.ds(pl.multiple_of(k * 8, 8), 8)
         two_edge[rows] = pack(lambda x, y: two_a[x + 2, y + 2, rows], qx, qy, 8)
-        go(two_moves(k))
+        go(two_moves(k), 3, at_two + k)
         return carry
 
     lax.fori_loop(0, pairs, pair_residue, 0)
 
     def step_two(k, carry):
-        arrive(two_moves(k))
+        arrive(two_moves(k), at_two + k)
         rows = pl.ds(pl.multiple_of(k * 8, 8), 8)
         ends = [join(lambda s, j=j: two_got[s, j, rows], 8) for j in range(5)]
         halo = sweep_edges(two_edge[rows], ends, r_edge(1, 8), qx, qy, 8, 0.03125)
@@ -421,7 +428,7 @@
                     + 0.03125 * r2_b[x + 1, y + 1] * total
                 )
         last_edge[rows] = pack(lambda x, y: two_c[x + 1, y + 1, rows], qx, qy, 4)
-        go(last_moves(k))
+        go(last_moves(k), 4, at_last + k)
         return carry
 
     lax.fori_loop(0, pairs, step_two, 0)
@@ -465,41 +472,31 @@
                             second[fx, fy, sl] = second[fx, fy, sl] + w
 
     def finish(k, carry):
-        arrive(last_moves(k))
+        arrive(last_moves(k), at_last + k)
         for half in range(2):
             step_last(k, half)
-            rows = pl.ds(pl.multiple_of((2 * k + half) * width, 8), width)
-
-            def line(x, c):
-                for y in range(ny):
-                    pltpu.make_async_copy(
-                        second.at[x, y, rows], out.at[rows, x, y], store_sem.at[2 * k + half]
-                    ).start()
-                return c
-
-            lax.fori_loop(0, nx, line, 0)
         return carry
 
     lax.fori_loop(0, pairs, finish, 0)
 
-    def drain(k, carry):
-        rows = pl.ds(pl.multiple_of(k * width, 8), width)
-        for p in (ORB, FIRST):
-            leave(fine_moves(p, k))
-        leave(one_moves(k))
-        whole = second.at[:, :, rows]
-        pltpu.make_async_copy(whole, whole, store_sem.at[k]).wait()
-        return carry
-
-    lax.fori_loop(0, chunks, drain, 0)
-
-    def drain_pair(k, carry):
-        leave(two_moves(k))
-        leave(last_moves(k))
-        return carry
-
-    lax.fori_loop(0, pairs, drain_pair, 0)
-    leave(r_moves())
+    leave(fine_moves(ORB, 0), chunks, 0)
+    leave(fine_moves(FIRST, 0), chunks, 1)
+    leave(one_moves(0), chunks, 2)
+    leave(two_moves(0), pairs, 3)
+    leave(last_moves(0), pairs, 4)
+    leave(r_moves(), 1, 5)
+
+
+def store(filtered, out, sem):
+    nx, ny = filtered.shape[:2]
+
+    def line(x, c):
+        for y in range(ny):
+            pltpu.make_async_copy(filtered.at[x, y], out.at[:, x, y], sem).start()
+        return c
+
+    lax.fori_loop(0, nx, line, 0)
+    pltpu.make_async_copy(filtered, filtered, sem).wait()
 
 
 def local(sizes, chunks, orbitals, potential, centre, half_width):
@@ -514,10 +511,8 @@
         return f32(nx // cut + 2 * halo, ny // cut + 2 * halo, bands if cut == 1 else bands // cut, nz)
 
     dma = pltpu.SemaphoreType.DMA
-    deep = 8 + 5 * sides
     scratch = [padded(1, 1)] * 2 + [padded(2, 2), padded(2, 1), padded(4, 2), padded(4, 1), padded(4, 1)]
     scratch += [
-        f32(nx, ny, bands, nz),
         f32(2, bands, nz),
         f32(2, sides, bands, nz),
         f32(bands // 2, nz),
@@ -536,27 +531,31 @@
         f32(5, 8, nz),
         f32(4 + sides, 8, nz),
         dma((chunks,)),
-        dma((chunks,)),
-        dma((2, 2, chunks, 4 + sides)),
-        dma((2, chunks, deep)),
-        dma((2, pairs, deep)),
-        dma((2, pairs, 4 + sides)),
-        dma((2, 4 + sides)),
+        dma((6,)),
+        dma((3 * chunks + 2 * pairs + 1,)),
+        f32((2 * (nx + ny) + sides) * bands // 8, 8, nz),
         pltpu.SMEM((bands,), jnp.float32),
         pltpu.SMEM((bands,), jnp.float32),
         f32(nx, ny, nz),
         dma((3,)),
     ]
-    return pl.pallas_call(
+    filtered = pl.pallas_call(
         functools.partial(kernel, sizes, chunks),
-        out_shape=jax.ShapeDtypeStruct(orbitals.shape, jnp.float32),
+        out_shape=pltpu.VMEM((nx, ny, bands, nz), jnp.float32),
         in_specs=[pl.BlockSpec(memory_space=pltpu.HBM)] * 4,
-        out_specs=pl.BlockSpec(memory_space=pl.ANY),
+        out_specs=pl.BlockSpec(memory_space=pltpu.VMEM),
         scratch_shapes=scratch,
         compiler_params=pltpu.CompilerParams(
             collective_id=0, has_side_effects=True, vmem_limit_bytes=48 * 1024 * 1024
         ),
     )(*(pltpu.with_memory_space_constraint(v, pltpu.HBM) for v in (centre, half_width, potential, orbitals)))
+    return pl.pallas_call(
+        store,
+        out_shape=jax.ShapeDtypeStruct(orbitals.shape, jnp.float32),
+        in_specs=[pl.BlockSpec(memory_space=pltpu.VMEM)],
+        out_specs=pl.BlockSpec(memory_space=pltpu.HBM),
+        scratch_shapes=[dma(())],
+    )(pltpu.with_memory_space_constraint(filtered, pltpu.VMEM))
 
 
 def solution(mesh):

time: 54.3 us -> 50.2 us (0.924)
  Pallas kernels: 52.7 us -> 49.9 us
  local copies, waits for them, and re-layouts: 1.32 us -> 0 us
    pallas_call x1 -> x2, Pallas kernels: 52.7 us -> 49.9 us  [the longest x1 48.6 us: local(): pl.pallas_call(functools.partial(kernel, sizes, chunks), out_shape=pltpu....]
    unnamed x1 -> x0, local copies, waits for them, and re-layouts: 1.32 us -> none
where the time goes in v2:
time: 50.2 us; the launch traced here: 49.9 us
  Pallas kernels  49.9 us (99%)
    pallas_call x1, Pallas kernels, local(): pl.pallas_call(functools.partial(kernel, sizes, chunks), out_shape=pltpu....  48.6 us
    pallas_call x1, Pallas kernels, local(): pl.pallas_call(store, out_shape=jax.ShapeDtypeStruct(orbitals.shape, jnp....  1.29 us

profile of v2, /device:TPU:0, one launch (start us, length us, event | category | flops | bytes accessed | tf_op | source)
XLA Modules:
  0.0 49.9 jit_solution(3308045306949764807)
XLA Ops:
  0.0 48.6 %shard_map.46.filtered = f32[8,8,64,128]{3,2,1,0:T(8,128)S(1)} custom-call(f32[64]{0:T(128)} %centre_in.1, f32[64]{0:T(128)} %half_width_in.1, f32[8,8,128]{2,1,0:T(8,128)} %pot_in.1, f32[64,8,8,128]{3,2,1,0:T(8,128)} %orbitals.1), custom_call_target="tpu_custom_call" | custom-call | tf_op jit(solution)/shard_map/pallas_call | solution.py:542
  48.7 1.3 %shard_map.47 = f32[64,8,8,128]{3,2,1,0:T(8,128)} custom-call(f32[8,8,64,128]{3,2,1,0:T(8,128)S(1)} %shard_map.46.filtered), custom_call_target="tpu_custom_call" | custom-call | tf_op jit(solution)/shard_map/pallas_call | solution.py:552

commit v3 on v2

--- a/solution.py
+++ b/solution.py
@@ -21,11 +21,12 @@
     one_edge, one_got, one_halo, two_edge, two_got, last_edge, last_got = scratch[9:16]
     band_a, band_i, pot_b, d1_b, r1_b, r2_b, r_sent, r_got = scratch[16:24]
     load_sem, send_sem, recv_sem, tally = scratch[24:28]
-    centre, half_width, pot, small_sem = scratch[28:32]
+    centre, half_width, pot, small_sem, token = scratch[28:33]
     bands, nx, ny, nz = second.shape[2], second.shape[0], second.shape[1], second.shape[3]
     width = bands // chunks
     groups = width // 8
     pairs = chunks // 2
+    early = chunks // 2
     mx, my, qx, qy = nx // 2, ny // 2, nx // 4, ny // 4
     sides = 2 if sizes["gz"] > 2 else 1
     at_one, at_two = 2 * chunks, 3 * chunks
@@ -38,12 +39,25 @@
         me, n = lax.axis_index(axis), sizes[axis]
         near[axis] = (lax.rem(me + n - 1, n), lax.rem(me + 1, n))
     zpeers = [near["gz"][1], near["gz"][0]][:sides]
-    peers = [{"gx": v} for v in near["gx"]] + [{"gy": v} for v in near["gy"]]
-    peers += [{"gz": v} for v in zpeers]
+    gy, ylast = lax.axis_index("gy"), sizes["gy"] - 1
+    peers = [{"gx": v} for v in near["gx"]] + [{"gz": v} for v in zpeers]
+
+    def signal(sem, to):
+        pl.semaphore_signal(sem, inc=1, device_id=to, device_id_type=MESH)
 
     barrier = pltpu.get_barrier_semaphore()
     for peer in peers:
-        pl.semaphore_signal(barrier, inc=1, device_id=peer, device_id_type=MESH)
+        signal(barrier, peer)
+
+    @pl.when(gy > 0)
+    def _():
+        signal(barrier, {"gy": gy - 1})
+
+    @pl.when(gy < ylast)
+    def _():
+        signal(barrier, {"gy": gy + 1})
+
+    ycount = lax.div(gy + ylast, ylast + 1) + lax.div(2 * ylast - gy, ylast + 1)
 
     smalls = [
         pltpu.make_async_copy(src, dst, small_sem.at[j])
@@ -54,19 +68,14 @@
     for small in smalls:
         small.start()
 
-    def loads(k):
-        rows = pl.ds(pl.multiple_of(k * width, 8), width)
-
-        def line(x, _):
-            for y in range(ny):
-                pltpu.make_async_copy(
-                    orbitals.at[rows, x, y], fine[ORB].at[x + 1, y + 1, rows], load_sem.at[k]
-                ).start()
-            return 0
-
-        lax.fori_loop(0, nx, line, 0)
-
-    lax.fori_loop(0, chunks, lambda k, c: (loads(k), c)[1], 0)
+    def load(x, c):
+        for y in range(ny):
+            pltpu.make_async_copy(
+                orbitals.at[:, x, y], fine[ORB].at[x + 1, y + 1], load_sem.at[0]
+            ).start()
+        return c
+
+    lax.fori_loop(0, nx, load, 0)
 
     def tiles(moves):
         return sum(math.prod(src.shape) for src, _, _ in moves) // (8 * nz)
@@ -85,6 +94,28 @@
                 device_id=to,
                 device_id_type=MESH,
             ).start()
+
+    def go_split(downs, ups, rest, sent, got):
+        @pl.when(gy == ylast)
+        def _():
+            go(ups + downs, sent, got)
+
+        @pl.when(gy != ylast)
+        def _():
+            go(downs + ups, sent, got)
+
+        go(rest, sent, got)
+
+    def go_faces(moves, sent, got):
+        go_split(moves[:1], moves[1:2], moves[2:], sent, got)
+
+    def go_deep(moves, sent, got):
+        downs, ups = [moves[0], *moves[4:6]], [moves[1], *moves[6:8]]
+        rest = moves[2:4]
+        for s in range(sides):
+            ends = moves[8 + 5 * s : 13 + 5 * s]
+            rest, ups, downs = rest + ends[:3], ups + ends[3:4], downs + ends[4:]
+        go_split(downs, ups, rest, sent, got)
 
     def arrive(moves, got):
         take(tiles(moves), recv_sem.at[got])
@@ -246,15 +277,59 @@
     def slab(k, i):
         return pl.ds(pl.multiple_of(k * width + i * 8, 8), 8)
 
-    def ready(k, carry):
-        rows = pl.ds(pl.multiple_of(k * width, 8), width)
-        whole = fine[ORB].at[pl.ds(1, nx), pl.ds(1, ny), rows]
-        pltpu.make_async_copy(whole, whole, load_sem.at[k]).wait()
-        return carry
-
-    lax.fori_loop(0, chunks, ready, 0)
-    pl.semaphore_wait(barrier, len(peers))
-    lax.fori_loop(0, chunks, lambda k, c: (go(fine_moves(ORB, k)[:4], 0, k), c)[1], 0)
+    pltpu.make_async_copy(
+        fine[ORB].at[pl.ds(1, nx), pl.ds(1, ny)],
+        fine[ORB].at[pl.ds(1, nx), pl.ds(1, ny)],
+        load_sem.at[0],
+    ).wait()
+    pl.semaphore_wait(barrier, len(peers) + ycount)
+
+    def start_near(k, carry):
+        down, up, *rest = fine_moves(ORB, k)
+
+        @pl.when(gy > 0)
+        def _():
+            go([down], 0, k)
+
+        @pl.when(gy < ylast)
+        def _():
+            go([up], 0, k)
+
+        go(rest[:2], 0, k)
+        return carry
+
+    def start_far(k, carry):
+        down, up, *_ = fine_moves(ORB, k)
+
+        @pl.when(gy == 0)
+        def _():
+            go([down], 0, k)
+
+        @pl.when(gy == ylast)
+        def _():
+            go([up], 0, k)
+
+        return carry
+
+    lax.fori_loop(0, early, start_near, 0)
+    for end, step, sem in ((0, 1, 0), (ylast, -1, 1)):
+        first, stop = end + step, ylast - end
+
+        @pl.when((gy != end) & (gy != first))
+        def _():
+            pl.semaphore_wait(token.at[sem], 1)
+
+        @pl.when((gy != end) & (gy != stop))
+        def _():
+            signal(token.at[sem], {"gy": gy + step})
+
+    lax.fori_loop(0, early, start_far, 0)
+
+    def start_all(k, carry):
+        start_far(k, carry)
+        return start_near(k, carry)
+
+    lax.fori_loop(early, chunks, start_all, 0)
 
     def start_z(k, carry):
         def inner(i, c):
@@ -322,7 +397,7 @@
             return c
 
         lax.fori_loop(0, groups, inner, 0)
-        go(fine_moves(FIRST, k), 1, chunks + k)
+        go_faces(fine_moves(FIRST, k), 1, chunks + k)
         return carry
 
     lax.fori_loop(0, chunks, step_first, 0)
@@ -369,7 +444,7 @@
 
         lax.fori_loop(0, groups, inner, 0)
         one_edge[packed] = pack(lambda x, y: one_a[x + 2, y + 2, packed], mx, my, 4)
-        go(one_moves(k), 2, at_one + k)
+        go_deep(one_moves(k), 2, at_one + k)
         return carry
 
     lax.fori_loop(0, chunks, step_second, 0)
@@ -406,7 +481,7 @@
         lax.fori_loop(2 * k, 2 * k + 2, step_residue, 0)
         rows = pl.ds(pl.multiple_of(k * 8, 8), 8)
         two_edge[rows] = pack(lambda x, y: two_a[x + 2, y + 2, rows], qx, qy, 8)
-        go(two_moves(k), 3, at_two + k)
+        go_deep(two_moves(k), 3, at_two + k)
         return carry
 
     lax.fori_loop(0, pairs, pair_residue, 0)
@@ -428,7 +503,7 @@
                     + 0.03125 * r2_b[x + 1, y + 1] * total
                 )
         last_edge[rows] = pack(lambda x, y: two_c[x + 1, y + 1, rows], qx, qy, 4)
-        go(last_moves(k), 4, at_last + k)
+        go_faces(last_moves(k), 4, at_last + k)
         return carry
 
     lax.fori_loop(0, pairs, step_two, 0)
@@ -530,7 +605,7 @@
         f32(nx // 4 + 2, ny // 4 + 2, 8, nz),
         f32(5, 8, nz),
         f32(4 + sides, 8, nz),
-        dma((chunks,)),
+        dma((1,)),
         dma((6,)),
         dma((3 * chunks + 2 * pairs + 1,)),
         f32((2 * (nx + ny) + sides) * bands // 8, 8, nz),
@@ -538,6 +613,7 @@
         pltpu.SMEM((bands,), jnp.float32),
         f32(nx, ny, nz),
         dma((3,)),
+        pltpu.SemaphoreType.REGULAR((2,)),
     ]
     filtered = pl.pallas_call(
         functools.partial(kernel, sizes, chunks),

time: 50.2 us -> 48.9 us (0.974)
  Pallas kernels: 49.9 us -> 48.7 us
    pallas_call x1, Pallas kernels: 48.6 us -> 47.4 us  [local(): pl.pallas_call(functools.partial(kernel, sizes, chunks), out_shape=pltpu....]
where the time goes in v3:
time: 48.9 us; the launch traced here: 48.7 us
  Pallas kernels  48.7 us (100%)
    pallas_call x1, Pallas kernels, local(): pl.pallas_call(functools.partial(kernel, sizes, chunks), out_shape=pltpu....  47.4 us
    pallas_call x1, Pallas kernels, local(): pl.pallas_call(store, out_shape=jax.ShapeDtypeStruct(orbitals.shape, jnp....  1.29 us

profile of v3, /device:TPU:0, one launch (start us, length us, event | category | flops | bytes accessed | tf_op | source)
XLA Modules:
  0.0 48.7 jit_solution(18022935720810291756)
XLA Ops:
  0.0 47.4 %shard_map.46.filtered = f32[8,8,64,128]{3,2,1,0:T(8,128)S(1)} custom-call(f32[64]{0:T(128)} %centre_in.1, f32[64]{0:T(128)} %half_width_in.1, f32[8,8,128]{2,1,0:T(8,128)} %pot_in.1, f32[64,8,8,128]{3,2,1,0:T(8,128)} %orbitals.1), custom_call_target="tpu_custom_call" | custom-call | tf_op jit(solution)/shard_map/pallas_call | solution.py:618
  47.4 1.3 %shard_map.47 = f32[64,8,8,128]{3,2,1,0:T(8,128)} custom-call(f32[8,8,64,128]{3,2,1,0:T(8,128)S(1)} %shard_map.46.filtered), custom_call_target="tpu_custom_call" | custom-call | tf_op jit(solution)/shard_map/pallas_call | solution.py:628

commit v4 on v3

--- a/solution.py
+++ b/solution.py
@@ -21,16 +21,18 @@
     one_edge, one_got, one_halo, two_edge, two_got, last_edge, last_got = scratch[9:16]
     band_a, band_i, pot_b, d1_b, r1_b, r2_b, r_sent, r_got = scratch[16:24]
     load_sem, send_sem, recv_sem, tally = scratch[24:28]
-    centre, half_width, pot, small_sem, token = scratch[28:33]
+    centre, half_width, pot, small_sem, token, relay_edge = scratch[28:34]
     bands, nx, ny, nz = second.shape[2], second.shape[0], second.shape[1], second.shape[3]
     width = bands // chunks
     groups = width // 8
     pairs = chunks // 2
     early = chunks // 2
+    relayed = 2 * (pairs - 1)
     mx, my, qx, qy = nx // 2, ny // 2, nx // 4, ny // 4
     sides = 2 if sizes["gz"] > 2 else 1
     at_one, at_two = 2 * chunks, 3 * chunks
     at_last, at_r = at_two + pairs, at_two + 2 * pairs
+    at_relay = at_r + 1
     lane = lax.broadcasted_iota(jnp.int32, (8, nz), 1)
     sub = lax.broadcasted_iota(jnp.int32, (8, nz), 0)
 
@@ -157,6 +159,26 @@
         for s, z in enumerate(zpeers):
             for j, to in enumerate([{}, {"gx": xp}, {"gx": xm}, {"gy": yp}, {"gy": ym}]):
                 moves.append((edge.at[rows], got.at[s, j, rows], {"gz": z, **to}))
+        return moves
+
+    def early_moves(k):
+        moves = one_moves(k)
+        keep = moves[:4]
+        for s in range(sides):
+            keep += moves[8 + 5 * s : 11 + 5 * s]
+        return keep
+
+    def relay_moves(k):
+        e = one_a
+        rows = pl.ds(pl.multiple_of(k * 8, 8), 8)
+        xm, xp = near["gx"]
+        moves = []
+        for y in (1, my + 2):
+            moves.append((e.at[2, y, rows], e.at[mx + 2, y, rows], {"gx": xm}))
+            moves.append((e.at[mx + 1, y, rows], e.at[1, y, rows], {"gx": xp}))
+        for s, z in enumerate(zpeers):
+            for j in (3, 4):
+                moves.append((relay_edge.at[rows], one_got.at[s, j, rows], {"gz": z}))
         return moves
 
     def last_moves(k):
@@ -381,7 +403,7 @@
     r_sent[4, pl.ds(0, 1)] = pack(lambda x, y: r1_b[x + 1, y + 1], mx, my, 4)[0:1]
     r_sent[4, pl.ds(1, 1)] = pack(lambda x, y: r2_b[x + 1, y + 1], qx, qy, 8)[0:1]
 
-    go(r_moves(), 5, at_r)
+    go(r_moves(), 7, at_r)
 
     def step_first(k, carry):
         arrive(fine_moves(ORB, k), k)
@@ -444,13 +466,38 @@
 
         lax.fori_loop(0, groups, inner, 0)
         one_edge[packed] = pack(lambda x, y: one_a[x + 2, y + 2, packed], mx, my, 4)
-        go_deep(one_moves(k), 2, at_one + k)
-        return carry
-
-    lax.fori_loop(0, chunks, step_second, 0)
+        return carry
+
+    def second_early(k, carry):
+        step_second(k, carry)
+        go_faces(early_moves(k), 2, at_one + k)
+        return carry
+
+    lax.fori_loop(0, relayed, second_early, 0)
+
+    def second_late(k, carry):
+        step_second(k, carry)
+        go_deep(one_moves(k), 3, at_one + k)
+        return carry
+
+    lax.fori_loop(relayed, chunks, second_late, 0)
+
+    def relay(k, carry):
+        arrive(early_moves(k), at_one + k)
+        rows = pl.ds(pl.multiple_of(k * 8, 8), 8)
+        spots = [(x, y) for x in range(mx) for y in (0, my - 1)]
+        acc = jnp.zeros((8, nz), jnp.float32)
+        for x, y in spots:
+            at = 8 * (x * my + y)
+            here = (lane >= at) & (lane < at + 8)
+            acc = jnp.where(here, roll(one_a[x + 2, my + 2 if y == 0 else 1, rows], at + 4), acc)
+        relay_edge[rows] = acc
+        go(relay_moves(k), 4, at_relay + k)
+        return carry
+
+    lax.fori_loop(0, relayed, relay, 0)
 
     def step_residue(k, carry):
-        arrive(one_moves(k), at_one + k)
         packed = pl.ds(pl.multiple_of(k * 8, 8), 8)
         rows = pl.ds(pl.multiple_of(lax.div(k, 2) * 8, 8), 8)
         mine = ((lane >> 1) & 1) == lax.rem(k, 2)
@@ -477,14 +524,31 @@
                 )
         return carry
 
-    def pair_residue(k, carry):
-        lax.fori_loop(2 * k, 2 * k + 2, step_residue, 0)
+    def residue_early(k, carry):
+        arrive(relay_moves(k), at_relay + k)
+        return step_residue(k, carry)
+
+    def send_two(k, carry):
         rows = pl.ds(pl.multiple_of(k * 8, 8), 8)
         two_edge[rows] = pack(lambda x, y: two_a[x + 2, y + 2, rows], qx, qy, 8)
-        go_deep(two_moves(k), 3, at_two + k)
-        return carry
-
-    lax.fori_loop(0, pairs, pair_residue, 0)
+        go_deep(two_moves(k), 5, at_two + k)
+        return carry
+
+    def pair_residue(k, carry):
+        lax.fori_loop(2 * k, 2 * k + 2, residue_early, 0)
+        return send_two(k, carry)
+
+    lax.fori_loop(0, relayed // 2, pair_residue, 0)
+
+    def residue_late(k, carry):
+        arrive(one_moves(k), at_one + k)
+        return step_residue(k, carry)
+
+    def pair_late(k, carry):
+        lax.fori_loop(2 * k, 2 * k + 2, residue_late, 0)
+        return send_two(k, carry)
+
+    lax.fori_loop(relayed // 2, pairs, pair_late, 0)
 
     def step_two(k, carry):
         arrive(two_moves(k), at_two + k)
@@ -503,7 +567,7 @@
                     + 0.03125 * r2_b[x + 1, y + 1] * total
                 )
         last_edge[rows] = pack(lambda x, y: two_c[x + 1, y + 1, rows], qx, qy, 4)
-        go_faces(last_moves(k), 4, at_last + k)
+        go_faces(last_moves(k), 6, at_last + k)
         return carry
 
     lax.fori_loop(0, pairs, step_two, 0)
@@ -556,10 +620,12 @@
 
     leave(fine_moves(ORB, 0), chunks, 0)
     leave(fine_moves(FIRST, 0), chunks, 1)
-    leave(one_moves(0), chunks, 2)
-    leave(two_moves(0), pairs, 3)
-    leave(last_moves(0), pairs, 4)
-    leave(r_moves(), 1, 5)
+    leave(early_moves(0), relayed, 2)
+    leave(one_moves(0), chunks - relayed, 3)
+    leave(relay_moves(0), relayed, 4)
+    leave(two_moves(0), pairs, 5)
+    leave(last_moves(0), pairs, 6)
+    leave(r_moves(), 1, 7)
 
 
 def store(filtered, out, sem):
@@ -606,14 +672,15 @@
         f32(5, 8, nz),
         f32(4 + sides, 8, nz),
         dma((1,)),
-        dma((6,)),
-        dma((3 * chunks + 2 * pairs + 1,)),
+        dma((8,)),
+        dma((4 * chunks + 2 * pairs,)),
         f32((2 * (nx + ny) + sides) * bands // 8, 8, nz),
         pltpu.SMEM((bands,), jnp.float32),
         pltpu.SMEM((bands,), jnp.float32),
         f32(nx, ny, nz),
         dma((3,)),
         pltpu.SemaphoreType.REGULAR((2,)),
+        f32(bands // 2, nz),
     ]
     filtered = pl.pallas_call(
         functools.partial(kernel, sizes, chunks),

time: 48.9 us -> 47.9 us (0.980)
  Pallas kernels: 48.7 us -> 47.7 us
    pallas_call x1, Pallas kernels: 47.4 us -> 46.4 us  [local(): pl.pallas_call(functools.partial(kernel, sizes, chunks), out_shape=pltpu....]
where the time goes in v4:
time: 47.9 us; the launch traced here: 47.7 us
  Pallas kernels  47.7 us (100%)
    pallas_call x1, Pallas kernels, local(): pl.pallas_call(functools.partial(kernel, sizes, chunks), out_shape=pltpu....  46.4 us
    pallas_call x1, Pallas kernels, local(): pl.pallas_call(store, out_shape=jax.ShapeDtypeStruct(orbitals.shape, jnp....  1.29 us

profile of v4, /device:TPU:0, one launch (start us, length us, event | category | flops | bytes accessed | tf_op | source)
XLA Modules:
  0.0 47.7 jit_solution(14865653709168529814)
XLA Ops:
  0.0 46.4 %shard_map.46.filtered = f32[8,8,64,128]{3,2,1,0:T(8,128)S(1)} custom-call(f32[64]{0:T(128)} %centre_in.1, f32[64]{0:T(128)} %half_width_in.1, f32[8,8,128]{2,1,0:T(8,128)} %pot_in.1, f32[64,8,8,128]{3,2,1,0:T(8,128)} %orbitals.1), custom_call_target="tpu_custom_call" | custom-call | tf_op jit(solution)/shard_map/pallas_call | solution.py:685
  46.4 1.3 %shard_map.47 = f32[64,8,8,128]{3,2,1,0:T(8,128)} custom-call(f32[8,8,64,128]{3,2,1,0:T(8,128)S(1)} %shard_map.46.filtered), custom_call_target="tpu_custom_call" | custom-call | tf_op jit(solution)/shard_map/pallas_call | solution.py:695

commit v5 on v3

--- a/solution.py
+++ b/solution.py
@@ -21,16 +21,18 @@
     one_edge, one_got, one_halo, two_edge, two_got, last_edge, last_got = scratch[9:16]
     band_a, band_i, pot_b, d1_b, r1_b, r2_b, r_sent, r_got = scratch[16:24]
     load_sem, send_sem, recv_sem, tally = scratch[24:28]
-    centre, half_width, pot, small_sem, token = scratch[28:33]
+    centre, half_width, pot, small_sem, token, one_c, sum_sent, sum_got = scratch[28:36]
     bands, nx, ny, nz = second.shape[2], second.shape[0], second.shape[1], second.shape[3]
     width = bands // chunks
     groups = width // 8
     pairs = chunks // 2
-    early = chunks // 2
+    early = 1
     mx, my, qx, qy = nx // 2, ny // 2, nx // 4, ny // 4
     sides = 2 if sizes["gz"] > 2 else 1
-    at_one, at_two = 2 * chunks, 3 * chunks
+    at_one = chunks + bands // 8
+    at_two = at_one + chunks
     at_last, at_r = at_two + pairs, at_two + 2 * pairs
+    at_swept = at_r + 1
     lane = lax.broadcasted_iota(jnp.int32, (8, nz), 1)
     sub = lax.broadcasted_iota(jnp.int32, (8, nz), 0)
 
@@ -95,7 +97,10 @@
                 device_id_type=MESH,
             ).start()
 
-    def go_split(downs, ups, rest, sent, got):
+    def go_far_first(moves, sent, got):
+        downs = [m for m in moves if m[2].get("gy") is near["gy"][0]]
+        ups = [m for m in moves if m[2].get("gy") is near["gy"][1]]
+
         @pl.when(gy == ylast)
         def _():
             go(ups + downs, sent, got)
@@ -104,18 +109,7 @@
         def _():
             go(downs + ups, sent, got)
 
-        go(rest, sent, got)
-
-    def go_faces(moves, sent, got):
-        go_split(moves[:1], moves[1:2], moves[2:], sent, got)
-
-    def go_deep(moves, sent, got):
-        downs, ups = [moves[0], *moves[4:6]], [moves[1], *moves[6:8]]
-        rest = moves[2:4]
-        for s in range(sides):
-            ends = moves[8 + 5 * s : 13 + 5 * s]
-            rest, ups, downs = rest + ends[:3], ups + ends[3:4], downs + ends[4:]
-        go_split(downs, ups, rest, sent, got)
+        go([m for m in moves if "gy" not in m[2]], sent, got)
 
     def arrive(moves, got):
         take(tiles(moves), recv_sem.at[got])
@@ -124,15 +118,9 @@
         take(times * tiles(moves), send_sem.at[sent])
 
     def fine_moves(p, k):
-        e = fine[p]
-        rows = pl.ds(pl.multiple_of(k * width, 8), width)
-        ys, xs = pl.ds(1, ny), pl.ds(1, nx)
-        moves = [
-            (e.at[xs, 1, rows], e.at[xs, ny + 1, rows], {"gy": near["gy"][0]}),
-            (e.at[xs, ny, rows], e.at[xs, 0, rows], {"gy": near["gy"][1]}),
-            (e.at[1, ys, rows], e.at[nx + 1, ys, rows], {"gx": near["gx"][0]}),
-            (e.at[nx, ys, rows], e.at[0, ys, rows], {"gx": near["gx"][1]}),
-        ]
+        n = (width, 8)[p]
+        rows = pl.ds(pl.multiple_of(k * n, 8), n)
+        moves = face_moves(fine[p], fine[p], k, n)
         for s, to in enumerate(zpeers):
             moves.append((zsend.at[p, rows], zrecv.at[p, s, rows], {"gz": to}))
         return moves
@@ -154,21 +142,59 @@
             (e.at[2, ay + 1, rows], e.at[ax + 2, 1, rows], {"gx": xm, "gy": yp}),
             (e.at[ax + 1, ay + 1, rows], e.at[1, 1, rows], {"gx": xp, "gy": yp}),
         ]
-        for s, z in enumerate(zpeers):
-            for j, to in enumerate([{}, {"gx": xp}, {"gx": xm}, {"gy": yp}, {"gy": ym}]):
-                moves.append((edge.at[rows], got.at[s, j, rows], {"gz": z, **to}))
-        return moves
+        return edge_moves(edge, got, rows) + moves[4:] + moves[:4]
+
+    def face_moves(src, dst, k, n):
+        rows = pl.ds(pl.multiple_of(k * n, 8), n)
+        ax, ay = src.shape[0] - 2, src.shape[1] - 2
+        ys, xs = pl.ds(1, ay), pl.ds(1, ax)
+        (xm, xp), (ym, yp) = near["gx"], near["gy"]
+        return [
+            (src.at[xs, 1, rows], dst.at[xs, ay + 1, rows], {"gy": ym}),
+            (src.at[xs, ay, rows], dst.at[xs, 0, rows], {"gy": yp}),
+            (src.at[1, ys, rows], dst.at[ax + 1, ys, rows], {"gx": xm}),
+            (src.at[ax, ys, rows], dst.at[0, ys, rows], {"gx": xp}),
+        ]
+
+    def edge_moves(edge, got, rows):
+        (xm, xp), (ym, yp) = near["gx"], near["gy"]
+        spread = [{}, {"gx": xp}, {"gx": xm}, {"gy": yp}, {"gy": ym}]
+        return [
+            (edge.at[rows], got.at[s, j, rows], {"gz": z, **to})
+            for s, z in enumerate(zpeers)
+            for j, to in enumerate(spread)
+        ]
+
+    def one_cells(k):
+        e = one_a
+        rows = pl.ds(pl.multiple_of(k * 8, 8), 8)
+        (xm, xp), (ym, yp) = near["gx"], near["gy"]
+        corners = [
+            (e.at[1, 1, rows], e.at[mx + 1, my + 1, rows], {"gx": xm, "gy": ym}),
+            (e.at[mx, 1, rows], e.at[0, my + 1, rows], {"gx": xp, "gy": ym}),
+            (e.at[1, my, rows], e.at[mx + 1, 0, rows], {"gx": xm, "gy": yp}),
+            (e.at[mx, my, rows], e.at[0, 0, rows], {"gx": xp, "gy": yp}),
+        ]
+        return corners + face_moves(e, e, k, 8)
+
+    def one_extras(k):
+        rows = pl.ds(pl.multiple_of(k * 8, 8), 8)
+        (xm, xp), (ym, yp) = near["gx"], near["gy"]
+        sums = [
+            (sum_sent.at[j, rows], sum_got.at[j, rows], to)
+            for j, to in ((1, {"gy": ym}), (0, {"gy": yp}), (3, {"gx": xm}), (2, {"gx": xp}))
+        ]
+        return edge_moves(one_edge, one_got, rows) + sums
+
+    def one_moves(k):
+        return one_extras(k)[:5 * sides] + one_cells(k) + one_extras(k)[5 * sides :]
+
+    def swept_moves(k):
+        return face_moves(one_b, one_c, k, 8)
 
     def last_moves(k):
-        e = two_c
         rows = pl.ds(pl.multiple_of(k * 8, 8), 8)
-        ys, xs = pl.ds(1, qy), pl.ds(1, qx)
-        moves = [
-            (e.at[xs, 1, rows], e.at[xs, qy + 1, rows], {"gy": near["gy"][0]}),
-            (e.at[xs, qy, rows], e.at[xs, 0, rows], {"gy": near["gy"][1]}),
-            (e.at[1, ys, rows], e.at[qx + 1, ys, rows], {"gx": near["gx"][0]}),
-            (e.at[qx, ys, rows], e.at[0, ys, rows], {"gx": near["gx"][1]}),
-        ]
+        moves = face_moves(two_c, two_c, k, 8)
         for s, to in enumerate(zpeers):
             moves.append((last_edge.at[rows], last_got.at[s, rows], {"gz": to}))
         return moves
@@ -183,9 +209,6 @@
         for s, to in enumerate(zpeers):
             moves.append((r_sent.at[4], r_got.at[4 + s], {"gz": to}))
         return moves
-
-    def one_moves(k):
-        return deep_moves(one_a, one_edge, one_got, k)
 
     def two_moves(k):
         return deep_moves(two_a, two_edge, two_got, k)
@@ -243,12 +266,13 @@
         cells += [(ax, y, xp, y) for y in range(ay)]
         cells += [(x, -1, ym, x * ay + ay - 1) for x in range(ax)]
         cells += [(x, ay, yp, x * ay) for x in range(ax)]
+        h = (src.shape[0] - ax) // 2
         for x, y, got, spot in cells:
-            c = src[x + 2, y + 2, rows]
-            total = (src[x + 1, y + 2, rows] + src[x + 3, y + 2, rows]) + (
-                src[x + 2, y + 1, rows] + src[x + 2, y + 3, rows]
-            )
-            total = total + along_z(c, edge_at(got, spot, w), w // 2)
+            c = src[x + h, y + h, rows]
+            total = along_z(c, edge_at(got, spot, w), w // 2)
+            for px, py in ((x - 1, y), (x + 1, y), (x, y - 1), (x, y + 1)):
+                if -h <= px < ax + h and -h <= py < ay + h:
+                    total = total + src[px + h, py + h, rows]
             dst[x + 1, y + 1, rows] = (2.0 - jacobi_weight) * c + coupling * r_at(x, y) * total
 
     def total_of(e, x, y, rows, h, w):
@@ -381,7 +405,7 @@
     r_sent[4, pl.ds(0, 1)] = pack(lambda x, y: r1_b[x + 1, y + 1], mx, my, 4)[0:1]
     r_sent[4, pl.ds(1, 1)] = pack(lambda x, y: r2_b[x + 1, y + 1], qx, qy, 8)[0:1]
 
-    go(r_moves(), 5, at_r)
+    go(r_moves(), 6, at_r)
 
     def step_first(k, carry):
         arrive(fine_moves(ORB, k), k)
@@ -394,10 +418,10 @@
                 v, total = around(ORB, sl, got, x)
                 fine[FIRST][x + 1, pl.ds(1, ny), sl] = ((pot_b[x] + a) * v - 0.5 * total) * f
             fine_pack(FIRST, sl)
+            go_far_first(fine_moves(FIRST, k * groups + i), 1, chunks + k * groups + i)
             return c
 
         lax.fori_loop(0, groups, inner, 0)
-        go_faces(fine_moves(FIRST, k), 1, chunks + k)
         return carry
 
     lax.fori_loop(0, chunks, step_first, 0)
@@ -420,10 +444,10 @@
         return join(lambda s: jnp.broadcast_to(r_got[4 + s, pl.ds(row, 1)], (8, nz)), w)
 
     def step_second(k, carry):
-        arrive(fine_moves(FIRST, k), chunks + k)
         packed = pl.ds(pl.multiple_of(k * 8, 8), 8)
 
         def inner(i, c):
+            arrive(fine_moves(FIRST, k * groups + i), chunks + k * groups + i)
             sl = slab(k, i)
             mine = (lane & 1) == i
             got = fine_edges(FIRST, sl)
@@ -437,17 +461,36 @@
                     both = v if both is None else both + v
                 for y2 in range(my):
                     s = 0.5 * pair_sum(both[2 * y2] + both[2 * y2 + 1], 1)
-                    one_a[x2 + 2, y2 + 2, packed] = jnp.where(
-                        mine, r1_b[x2 + 1, y2 + 1] * s, one_a[x2 + 2, y2 + 2, packed]
+                    one_a[x2 + 1, y2 + 1, packed] = jnp.where(
+                        mine, r1_b[x2 + 1, y2 + 1] * s, one_a[x2 + 1, y2 + 1, packed]
                     )
             return c
 
         lax.fori_loop(0, groups, inner, 0)
-        one_edge[packed] = pack(lambda x, y: one_a[x + 2, y + 2, packed], mx, my, 4)
-        go_deep(one_moves(k), 2, at_one + k)
+        one_edge[packed] = pack(lambda x, y: one_a[x + 1, y + 1, packed], mx, my, 4)
+        for j, outer, inner_cell in (
+            (1, lambda i: (i, 0), lambda i: (i, 1)),
+            (0, lambda i: (i, my - 1), lambda i: (i, my - 2)),
+            (3, lambda i: (0, i), lambda i: (1, i)),
+            (2, lambda i: (mx - 1, i), lambda i: (mx - 2, i)),
+        ):
+            halves = []
+            for pair in range(2):
+                acc = None
+                for i in (2 * pair, 2 * pair + 1):
+                    (ox, oy), (ix, iy) = outer(i), inner_cell(i)
+                    v = r1_b[ox + 1, oy + 1] * one_a[ix + 1, iy + 1, packed]
+                    acc = v if acc is None else acc + v
+                halves.append(pair_sum(acc, 2))
+            sum_sent[j, packed] = jnp.where((lane & 2) == 0, *halves)
+        go_far_first(one_moves(k), 2, at_one + k)
         return carry
 
     lax.fori_loop(0, chunks, step_second, 0)
+
+    def spread(v, half):
+        left = (lane & 2) == 0
+        return jnp.where(left, v, roll(v, 2)) if half == 0 else jnp.where(left, roll(v, -2), v)
 
     def step_residue(k, carry):
         arrive(one_moves(k), at_one + k)
@@ -468,10 +511,14 @@
                         h = edge_at(halo, x * my + y, 4)
                         c, total = total_of(one_b, x, y, packed, h, 2)
                         d = d1_b[x, y]
-                        source = one_a[x + 2, y + 2, packed] * (d * (1.0 / jacobi_weight))
+                        source = one_a[x + 1, y + 1, packed] * (d * (1.0 / jacobi_weight))
                         v = source - d * c + 0.125 * total
                         acc = v if acc is None else acc + v
-                s = 0.5 * pair_sum(acc, 2)
+                acc = pair_sum(acc, 2)
+                for j, near_face, i in ((0, y2 == 0, x2), (1, y2 == qy - 1, x2), (2, x2 == 0, y2), (3, x2 == qx - 1, y2)):
+                    if near_face:
+                        acc = acc + 0.125**2 * spread(sum_got[j, packed], i)
+                s = 0.5 * acc
                 two_a[x2 + 2, y2 + 2, rows] = jnp.where(
                     mine, r2_b[x2 + 1, y2 + 1] * s, two_a[x2 + 2, y2 + 2, rows]
                 )
@@ -481,7 +528,9 @@
         lax.fori_loop(2 * k, 2 * k + 2, step_residue, 0)
         rows = pl.ds(pl.multiple_of(k * 8, 8), 8)
         two_edge[rows] = pack(lambda x, y: two_a[x + 2, y + 2, rows], qx, qy, 8)
-        go_deep(two_moves(k), 3, at_two + k)
+        go_far_first(two_moves(k), 3, at_two + k)
+        for half in range(2):
+            go_far_first(swept_moves(2 * k + half), 4, at_swept + 2 * k + half)
         return carry
 
     lax.fori_loop(0, pairs, pair_residue, 0)
@@ -503,7 +552,7 @@
                     + 0.03125 * r2_b[x + 1, y + 1] * total
                 )
         last_edge[rows] = pack(lambda x, y: two_c[x + 1, y + 1, rows], qx, qy, 4)
-        go_faces(last_moves(k), 4, at_last + k)
+        go_far_first(last_moves(k), 5, at_last + k)
         return carry
 
     lax.fori_loop(0, pairs, step_two, 0)
@@ -511,24 +560,20 @@
     def step_last(k, half):
         rows = pl.ds(pl.multiple_of(k * 8, 8), 8)
         packed = pl.ds(pl.multiple_of(k * 16 + half * 8, 8), 8)
-        left = (lane & 2) == 0
-
-        def spread(v):
-            return jnp.where(left, v, roll(v, 2)) if half == 0 else jnp.where(left, roll(v, -2), v)
-
         coarse = {}
         for x in range(-1, qx + 1):
             for y in range(-1, qy + 1):
                 if 0 <= x < qx or 0 <= y < qy:
-                    coarse[x, y] = spread(two_c[x + 1, y + 1, rows])
+                    coarse[x, y] = spread(two_c[x + 1, y + 1, rows], half)
         got = join(lambda s: last_got[s, rows], 4)
         ends = {
-            (x, y): spread(edge_at(got, x * qy + y, 4)) for x in range(qx) for y in range(qy)
+            (x, y): spread(edge_at(got, x * qy + y, 4), half) for x in range(qx) for y in range(qy)
         }
         halo = one_halo[packed]
 
         def at(x, y):
-            return one_b[x + 1, y + 1, packed] + coarse[(x + 2) // 2 - 1, (y + 2) // 2 - 1]
+            e = one_b if 0 <= x < mx and 0 <= y < my else one_c
+            return e[x + 1, y + 1, packed] + coarse[(x + 2) // 2 - 1, (y + 2) // 2 - 1]
 
         for x in range(mx):
             for y in range(my):
@@ -536,7 +581,7 @@
                 total = (at(x - 1, y) + at(x + 1, y)) + (at(x, y - 1) + at(x, y + 1))
                 h = edge_at(halo, x * my + y, 4) + ends[x // 2, y // 2]
                 total = total + along_z(c, h, 2)
-                v = (1.0 - jacobi_weight) * c + one_a[x + 2, y + 2, packed]
+                v = (1.0 - jacobi_weight) * c + one_a[x + 1, y + 1, packed]
                 v = v + 0.125 * r1_b[x + 1, y + 1] * total
                 odd = (lane & 1) == 1
                 for i, w in enumerate((jnp.where(odd, roll(v, 1), v), jnp.where(odd, v, roll(v, -1)))):
@@ -549,28 +594,27 @@
     def finish(k, carry):
         arrive(last_moves(k), at_last + k)
         for half in range(2):
+            arrive(swept_moves(2 * k + half), at_swept + 2 * k + half)
             step_last(k, half)
         return carry
 
     lax.fori_loop(0, pairs, finish, 0)
 
     leave(fine_moves(ORB, 0), chunks, 0)
-    leave(fine_moves(FIRST, 0), chunks, 1)
+    leave(fine_moves(FIRST, 0), bands // 8, 1)
     leave(one_moves(0), chunks, 2)
     leave(two_moves(0), pairs, 3)
-    leave(last_moves(0), pairs, 4)
-    leave(r_moves(), 1, 5)
+    leave(swept_moves(0), chunks, 4)
+    leave(last_moves(0), pairs, 5)
+    leave(r_moves(), 1, 6)
 
 
 def store(filtered, out, sem):
     nx, ny = filtered.shape[:2]
 
-    def line(x, c):
+    for x in range(nx):
         for y in range(ny):
             pltpu.make_async_copy(filtered.at[x, y], out.at[:, x, y], sem).start()
-        return c
-
-    lax.fori_loop(0, nx, line, 0)
     pltpu.make_async_copy(filtered, filtered, sem).wait()
 
 
@@ -586,7 +630,7 @@
         return f32(nx // cut + 2 * halo, ny // cut + 2 * halo, bands if cut == 1 else bands // cut, nz)
 
     dma = pltpu.SemaphoreType.DMA
-    scratch = [padded(1, 1)] * 2 + [padded(2, 2), padded(2, 1), padded(4, 2), padded(4, 1), padded(4, 1)]
+    scratch = [padded(1, 1)] * 2 + [padded(2, 1), padded(2, 1), padded(4, 2), padded(4, 1), padded(4, 1)]
     scratch += [
         f32(2, bands, nz),
         f32(2, sides, bands, nz),
@@ -606,14 +650,17 @@
         f32(5, 8, nz),
         f32(4 + sides, 8, nz),
         dma((1,)),
-        dma((6,)),
-        dma((3 * chunks + 2 * pairs + 1,)),
+        dma((7,)),
+        dma((3 * chunks + bands // 8 + 2 * pairs + 1,)),
         f32((2 * (nx + ny) + sides) * bands // 8, 8, nz),
         pltpu.SMEM((bands,), jnp.float32),
         pltpu.SMEM((bands,), jnp.float32),
         f32(nx, ny, nz),
         dma((3,)),
         pltpu.SemaphoreType.REGULAR((2,)),
+        padded(2, 1),
+        f32(4, bands // 2, nz),
+        f32(4, bands // 2, nz),
     ]
     filtered = pl.pallas_call(
         functools.partial(kernel, sizes, chunks),

time: 48.9 us -> 47 us (0.961)
  Pallas kernels: 48.7 us -> 46.8 us
    pallas_call x1, Pallas kernels: 47.4 us -> 45.5 us  [local(): pl.pallas_call(functools.partial(kernel, sizes, chunks), out_shape=pltpu....]
where the time goes in v5:
time: 47 us; the launch traced here: 46.8 us
  Pallas kernels  46.8 us (100%)
    pallas_call x1, Pallas kernels, local(): pl.pallas_call(functools.partial(kernel, sizes, chunks), out_shape=pltpu....  45.5 us
    pallas_call x1, Pallas kernels, local(): pl.pallas_call(store, out_shape=jax.ShapeDtypeStruct(orbitals.shape, jnp....  1.29 us

profile of v5, /device:TPU:0, one launch (start us, length us, event | category | flops | bytes accessed | tf_op | source)
XLA Modules:
  0.0 46.8 jit_solution(1628929584853629582)
XLA Ops:
  0.0 45.5 %shard_map.46.filtered = f32[8,8,64,128]{3,2,1,0:T(8,128)S(1)} custom-call(f32[64]{0:T(128)} %centre_in.1, f32[64]{0:T(128)} %half_width_in.1, f32[8,8,128]{2,1,0:T(8,128)} %pot_in.1, f32[64,8,8,128]{3,2,1,0:T(8,128)} %orbitals.1), custom_call_target="tpu_custom_call" | custom-call | tf_op jit(solution)/shard_map/pallas_call | solution.py:665
  45.5 1.3 %shard_map.47 = f32[64,8,8,128]{3,2,1,0:T(8,128)} custom-call(f32[8,8,64,128]{3,2,1,0:T(8,128)S(1)} %shard_map.46.filtered), custom_call_target="tpu_custom_call" | custom-call | tf_op jit(solution)/shard_map/pallas_call | solution.py:675

commit v6 on v5

--- a/solution.py
+++ b/solution.py
@@ -529,11 +529,12 @@
         rows = pl.ds(pl.multiple_of(k * 8, 8), 8)
         two_edge[rows] = pack(lambda x, y: two_a[x + 2, y + 2, rows], qx, qy, 8)
         go_far_first(two_moves(k), 3, at_two + k)
-        for half in range(2):
-            go_far_first(swept_moves(2 * k + half), 4, at_swept + 2 * k + half)
         return carry
 
     lax.fori_loop(0, pairs, pair_residue, 0)
+    lax.fori_loop(
+        0, chunks, lambda k, c: (go_far_first(swept_moves(k), 4, at_swept + k), c)[1], 0
+    )
 
     def step_two(k, carry):
         arrive(two_moves(k), at_two + k)

time: 47 us -> 47 us (level)
  no operation moved by 1% of the time
where the time goes in v6:
time: 47 us; the launch traced here: 46.8 us
  Pallas kernels  46.8 us (100%)
    pallas_call x1, Pallas kernels, local(): pl.pallas_call(functools.partial(kernel, sizes, chunks), out_shape=pltpu....  45.5 us
    pallas_call x1, Pallas kernels, local(): pl.pallas_call(store, out_shape=jax.ShapeDtypeStruct(orbitals.shape, jnp....  1.29 us

profile of v6, /device:TPU:0, one launch (start us, length us, event | category | flops | bytes accessed | tf_op | source)
XLA Modules:
  0.0 46.8 jit_solution(2128601655242069046)
XLA Ops:
  0.0 45.5 %shard_map.46.filtered = f32[8,8,64,128]{3,2,1,0:T(8,128)S(1)} custom-call(f32[64]{0:T(128)} %centre_in.1, f32[64]{0:T(128)} %half_width_in.1, f32[8,8,128]{2,1,0:T(8,128)} %pot_in.1, f32[64,8,8,128]{3,2,1,0:T(8,128)} %orbitals.1), custom_call_target="tpu_custom_call" | custom-call | tf_op jit(solution)/shard_map/pallas_call | solution.py:666
  45.5 1.3 %shard_map.47 = f32[64,8,8,128]{3,2,1,0:T(8,128)} custom-call(f32[8,8,64,128]{3,2,1,0:T(8,128)S(1)} %shard_map.46.filtered), custom_call_target="tpu_custom_call" | custom-call | tf_op jit(solution)/shard_map/pallas_call | solution.py:676
